TPU v7x, 8 devices: a whole 2x2x1 slice. The times are simulated.
8 devices in a mesh: stage: 1 (over z), data: 8 (over y, x, core).
Axes of the slice: x: 2, y: 2, z: 1, core: 2. Of those that a mesh axis runs over, the one named last changes fastest.
Arguments:
- w_master: float32 [128, 512, 512], P('stage', 'data')
- momentum: float32 [128, 512, 512], P('stage', 'data')
- grads: bfloat16 [8, 128, 512, 512], P(('stage', 'data'))
Outputs:
- output 1: float32 [128, 512, 512], P('stage', 'data')
- output 2: float32 [128, 512, 512], P('stage', 'data')
All inputs are finite; a program needn't handle non-finite values.
Results may differ from a plain program's by a relative error of at most 0.0146391.
Values are sent between devices in bfloat16 or wider.
A program may use at most 1 GiB of HBM per device.

v0:
```python
import functools
import math

import jax
import jax.numpy as jnp
from jax import lax
from jax.experimental import pallas as pl
from jax.experimental.pallas import tpu as pltpu
from jax.sharding import PartitionSpec as P

MOMENTUM_COEF = 0.95
LEARN_RATE = 0.05
WEIGHT_DECAY = 0.2
NORM_EPS = 1e-7
COEF_A = 3.4445
COEF_B = -4.7750
COEF_C = 2.0315
NS_ITERS = 5

NDEV = 8
CHUNK = 8
HALF = 4
AHEAD = 2
SLOTS = 3
XSLOTS = 5
HOLD = 2
RSLOTS = 6
PIECES = 4
MESH = pl.DeviceIdType.MESH


def muon_kernel(
    grad, mom, w, results, raw,
    inbuf, kept, part, momb, stage, owned, nstage, owned_n, xbuf, xin, gram, poly,
    raw_s, raw_r, part_s, part_r, own_s, own_r, nrm_s, nrm_r, back_s, back_r,
    in_sem, mom_in, w_in,
):
    n_mats, rows, cols = mom.shape
    rms_scale = 0.2 * math.sqrt(max(rows * NDEV, cols))
    w_out, mom_out = results.at[0], results.at[1]
    steps = n_mats // CHUNK
    me = lax.axis_index("data")
    y, x, c = me // 4, (me // 2) % 2, me % 2
    partner = y * 4 + x * 2 + (1 - c)
    x_nbr = y * 4 + (1 - x) * 2
    y_nbr = (1 - y) * 4 + x * 2

    def remote(src, dst, send, recv, dev):
        return pltpu.make_async_remote_copy(
            src_ref=src, dst_ref=dst, send_sem=send, recv_sem=recv,
            device_id={"data": dev}, device_id_type=MESH)

    barrier = pltpu.get_barrier_semaphore()
    for r in range(1, NDEV):
        pl.semaphore_signal(barrier, inc=1, device_id={"data": (me + r) % NDEV}, device_id_type=MESH)
    pl.semaphore_wait(barrier, NDEV - 1)

    def raw_copies(k):
        a = pl.ds(k * CHUNK, HALF)
        b = pl.ds(k * CHUNK + HALF, HALF)
        out = []
        for dc in range(2):
            out.append(remote(grad.at[a, :, 1 - x, dc], raw.at[k, 0, 1 + c],
                              raw_s.at[k, 0, 1 + dc], raw_r.at[k, 0, 1 + c], x_nbr + dc))
            out.append(remote(grad.at[b, 1 - y, :, dc], raw.at[k, 1, 1 + c],
                              raw_s.at[k, 1, 1 + dc], raw_r.at[k, 1, 1 + c], y_nbr + dc))
        out.append(remote(grad.at[a, :, x, 1 - c], raw.at[k, 0, 0], raw_s.at[k, 0, 0], raw_r.at[k, 0, 0], partner))
        out.append(remote(grad.at[b, y, :, 1 - c], raw.at[k, 1, 0], raw_s.at[k, 1, 0], raw_r.at[k, 1, 0], partner))
        return out

    def raw_arrival(k, s, i):
        return pltpu.make_async_copy(raw.at[k, s, i], raw.at[k, s, i], raw_r.at[k, s, i])

    def own_copy(k, s):
        if s == 0:
            src = grad.at[pl.ds(k * CHUNK, HALF), :, x, c]
        else:
            src = grad.at[pl.ds(k * CHUNK + HALF, HALF), y, :, c]
        return pltpu.make_async_copy(src, inbuf.at[s, 0], in_sem.at[s, 0])

    def raw_load(k, s, i):
        return pltpu.make_async_copy(raw.at[k, s, i], inbuf.at[s, 1 + i], in_sem.at[s, 1 + i])

    def part_copy(k, s):
        slot = k % SLOTS
        return remote(part.at[slot, s], mom_out.at[pl.ds(k * CHUNK + s * HALF, HALF)],
                      part_s.at[slot, s], part_r.at[k, s], (y_nbr if s == 0 else x_nbr) + c)

    def mom_load(k):
        return pltpu.make_async_copy(mom.at[pl.ds(k * CHUNK, CHUNK)], momb.at[k % SLOTS], mom_in.at[k % SLOTS])

    def w_load(k):
        rng = pl.ds(k * CHUNK, CHUNK)
        return pltpu.make_async_copy(w.at[rng], w_out.at[rng], w_in.at[k])

    def own_send(k, r):
        j = (me + r) % NDEV
        slot = k % SLOTS
        return remote(stage.at[slot, j], owned.at[k % RSLOTS, pl.ds(me * rows, rows)],
                      own_s.at[slot, r], own_r.at[k, r], j)

    def nrm_send(k, r):
        j = (me + r) % NDEV
        slot = k % SLOTS
        return remote(nstage.at[slot, j], owned_n.at[k, me], nrm_s.at[slot, r], nrm_r.at[k, r], j)

    def back_send(k, r):
        j = (me + r) % NDEV
        slot = k % XSLOTS
        return remote(xbuf.at[slot, pl.ds(j * rows, rows)], xin.at[k % RSLOTS, me],
                      back_s.at[slot, r], back_r.at[k, r], j)

    def sum_chunk(k):
        slot = k % SLOTS
        for s in range(2):
            for i in range(3):
                raw_arrival(k, s, i).wait()
                raw_load(k, s, i).start()

        @pl.when(k >= SLOTS)
        def _():
            for s in range(2):
                part_copy(k - SLOTS, s).wait_send()

        for s in range(2):
            own_copy(k, s).wait()
            for i in range(3):
                raw_load(k, s, i).wait()
            keep = y if s == 0 else x

            @pl.loop(0, HALF)
            def _(m):
                def total(e):
                    v = [inbuf[s, i, m, e].astype(jnp.float32) for i in range(4)]
                    return (v[0] + v[1]) + (v[2] + v[3])

                part[slot, s, m] = total(1 - keep)
                kept[k % 2, s * HALF + m] = total(keep)

            part_copy(k, s).start()

        @pl.when(k + 1 < steps)
        def _():
            for s in range(2):
                own_copy(k + 1, s).start()
        w_load(k).start()

    def finish_chunk(k):
        slot = k % SLOTS
        mom_load(k).wait()
        for s in range(2):
            part_copy(k, s).wait_recv()

        @pl.when(k >= SLOTS)
        def _():
            for r in range(1, NDEV):
                own_send(k - SLOTS, r).wait_send()
                nrm_send(k - SLOTS, r).wait_send()

        @pl.loop(0, CHUNK)
        def _(j):
            new = MOMENTUM_COEF * momb[slot, j] + (kept[k % 2, j] + mom_out[k * CHUNK + j])
            mom_out[k * CHUNK + j] = new
            stage[slot, j] = new.astype(jnp.bfloat16)
            sq = jnp.sum(new * new, axis=0, keepdims=True)
            nstage[slot, j] = (sq[:, :128] + sq[:, 128:256]) + (sq[:, 256:384] + sq[:, 384:])

        for r in range(1, NDEV):
            own_send(k, r).start()
            nrm_send(k, r).start()
        owned[k % RSLOTS, pl.ds(pl.multiple_of(me * rows, rows), rows)] = stage[slot, me]
        owned_n[k, me] = nstage[slot, me]

        @pl.when(k + 1 < steps)
        def _():
            mom_load(k + 1).start()

    def orthogonalize(k):
        slot = k % XSLOTS

        @pl.when(k >= XSLOTS)
        def _():
            for r in range(1, NDEV):
                back_send(k - XSLOTS, r).wait_send()

        for r in range(1, NDEV):
            own_send(k, r).wait_recv()
            nrm_send(k, r).wait_recv()
        sq = jnp.sum(owned_n[k], axis=0)
        nrm = jnp.sqrt(jnp.sum(sq, axis=1, keepdims=True))
        den = nrm + NORM_EPS

        @pl.loop(0, NDEV)
        def _(i):
            blk = pl.ds(pl.multiple_of(i * rows, rows), rows)
            xbuf[slot, blk] = (owned[k % RSLOTS, blk].astype(jnp.float32) / den).astype(jnp.bfloat16)

        @pl.loop(0, NS_ITERS)
        def _(_):
            cur = xbuf[slot]
            gram[...] = lax.dot_general(cur, cur, (((1,), (1,)), ((), ())),
                                        preferred_element_type=jnp.float32).astype(jnp.bfloat16)
            g = gram[...]
            sqr = jnp.dot(g, g, preferred_element_type=jnp.float32)
            poly[...] = (COEF_B * g.astype(jnp.float32) + COEF_C * sqr).astype(jnp.bfloat16)
            px = jnp.dot(poly[...], cur, preferred_element_type=jnp.float32)
            xbuf[slot] = (COEF_A * cur.astype(jnp.float32) + px).astype(jnp.bfloat16)

        xin[k % RSLOTS, me] = xbuf[slot, pl.ds(pl.multiple_of(me * rows, rows), rows)]

    def send_back(k):
        for r in range(1, NDEV):
            back_send(k, r).start()

    def update_weights(k):
        w_load(k).wait()
        for r in range(1, NDEV):
            j = (me + NDEV - r) % NDEV
            pltpu.make_async_copy(xin.at[k % RSLOTS, j], xin.at[k % RSLOTS, j], back_r.at[k, r]).wait()

        @pl.loop(0, CHUNK)
        def _(j):
            old = w_out[k * CHUNK + j]
            step = xin[k % RSLOTS, j].astype(jnp.float32) * rms_scale
            w_out[k * CHUNK + j] = old - LEARN_RATE * (step + WEIGHT_DECAY * old)

    for k in range(AHEAD):
        for copy in raw_copies(k):
            copy.start()
    for s in range(2):
        own_copy(0, s).start()
    mom_load(0).start()

    @pl.loop(0, steps)
    def _(t):
        @pl.when(t + AHEAD < steps)
        def _():
            for copy in raw_copies(t + AHEAD):
                copy.start()

        sum_chunk(t)

        @pl.when(t >= 2 + HOLD)
        def _():
            send_back(t - 2 - HOLD)

        @pl.when(t >= 1)
        def _():
            finish_chunk(t - 1)

        @pl.when(t >= 2)
        def _():
            orthogonalize(t - 2)

        @pl.when(t >= 4 + HOLD)
        def _():
            update_weights(t - 4 - HOLD)

    last = steps - 1
    send_back(last - 3)
    finish_chunk(last)
    send_back(last - 2)
    orthogonalize(last - 1)
    send_back(last - 1)
    orthogonalize(last)
    send_back(last)

    @pl.loop(steps - 4 - HOLD, steps)
    def _(k):
        update_weights(k)

    @pl.loop(0, steps)
    def _(k):
        for copy in raw_copies(k):
            copy.wait_send()

    @pl.loop(steps - SLOTS, steps)
    def _(k):
        for s in range(2):
            part_copy(k, s).wait_send()
        for r in range(1, NDEV):
            own_send(k, r).wait_send()
            nrm_send(k, r).wait_send()

    @pl.loop(steps - XSLOTS, steps)
    def _(k):
        for r in range(1, NDEV):
            back_send(k, r).wait_send()


def write_kernel(results, w_out, mom_out, sems):
    n = w_out.shape[0] // PIECES
    copies = []
    for i in range(PIECES):
        rng = pl.ds(i * n, n)
        copies.append(pltpu.make_async_copy(results.at[0, rng], w_out.at[rng], sems.at[0, i]))
        copies.append(pltpu.make_async_copy(results.at[1, rng], mom_out.at[rng], sems.at[1, i]))
    for copy in copies:
        copy.start()
    for copy in copies:
        copy.wait()


def solution(mesh):
    row_spec = P('stage', 'data', None)
    grad_spec = P(('stage', 'data'), None, None, None)

    def local_step(w_rows, mom_rows, grad_full):
        n_mats, rows, n_cols = w_rows.shape
        n_rows = rows * NDEV
        steps = n_mats // CHUNK
        grad_view = grad_full.reshape(n_mats, 2, 2, 2, rows, n_cols)
        f32, bf16 = jnp.float32, jnp.bfloat16
        dma = pltpu.SemaphoreType.DMA
        hbm = pl.BlockSpec(memory_space=pltpu.HBM)
        vmem = pl.BlockSpec(memory_space=pltpu.VMEM)
        results, _ = pl.pallas_call(
            muon_kernel,
            name="muon_step",
            out_shape=(
                pltpu.VMEM((2, n_mats, rows, n_cols), f32),
                jax.ShapeDtypeStruct((steps, 2, 3, HALF, 2, rows, n_cols), bf16),
            ),
            in_specs=[hbm] * 3,
            out_specs=(vmem, hbm),
            scratch_shapes=[
                pltpu.VMEM((2, 4, HALF, 2, rows, n_cols), bf16),
                pltpu.VMEM((2, CHUNK, rows, n_cols), f32),
                pltpu.VMEM((SLOTS, 2, HALF, rows, n_cols), f32),
                pltpu.VMEM((SLOTS, CHUNK, rows, n_cols), f32),
                pltpu.VMEM((SLOTS, CHUNK, rows, n_cols), bf16),
                pltpu.VMEM((RSLOTS, n_rows, n_cols), bf16),
                pltpu.VMEM((SLOTS, CHUNK, 1, 128), f32),
                pltpu.VMEM((steps, NDEV, 1, 128), f32),
                pltpu.VMEM((XSLOTS, n_rows, n_cols), bf16),
                pltpu.VMEM((RSLOTS, CHUNK, rows, n_cols), bf16),
                pltpu.VMEM((n_rows, n_rows), bf16),
                pltpu.VMEM((n_rows, n_rows), bf16),
                dma((steps, 2, 3)), dma((steps, 2, 3)),
                dma((SLOTS, 2)), dma((steps, 2)),
                dma((SLOTS, NDEV)), dma((steps, NDEV)),
                dma((SLOTS, NDEV)), dma((steps, NDEV)),
                dma((XSLOTS, NDEV)), dma((steps, NDEV)),
                dma((2, 4)), dma((SLOTS,)), dma((steps,)),
            ],
            compiler_params=pltpu.CompilerParams(
                collective_id=0, has_side_effects=True, vmem_limit_bytes=31 * 2 ** 20),
        )(grad_view, mom_rows, w_rows)
        return pl.pallas_call(
            write_kernel,
            name="write_results",
            out_shape=(jax.ShapeDtypeStruct(w_rows.shape, f32), jax.ShapeDtypeStruct(w_rows.shape, f32)),
            in_specs=[vmem],
            out_specs=(hbm, hbm),
            scratch_shapes=[dma((2, PIECES))],
            compiler_params=pltpu.CompilerParams(vmem_limit_bytes=2 ** 20),
        )(results)

    return jax.shard_map(local_step, mesh=mesh, in_specs=(row_spec, row_spec, grad_spec),
                         out_specs=(row_spec, row_spec), check_vma=False)
```

profile of v0, /device:TPU:0, one launch (start us, length us, event | category | flops | bytes accessed | tf_op | source)
XLA Modules:
  0.0 745.0 jit_solution(6678697104060108247)
XLA Ops:
  0.6 733.3 %muon_step.1 = (f32[2,128,64,512]{3,2,1,0:T(8,128)S(1)}, bf16[16,2,3,4,2,64,512]{6,5,4,3,2,1,0:T(8,128)(2,1)}) custom-call(bf16[128,2,2,2,64,512]{5,4,3,2,1,0:T(8,128)(2,1)} %bitcast.grad, f32[128,64,512]{2,1,0:T(8,128)} %mom.1, f32[128,64,512]{2,1,0:T(8,128)} %w.1), custom_call_target="tpu_custom_call" | custom-call | tf_op jit(solution)/shard_map/muon_step/pallas_call | solution.py:317
  734.0 11.0 %write_results.1 = (f32[128,64,512]{2,1,0:T(8,128)}, f32[128,64,512]{2,1,0:T(8,128)}) custom-call(f32[2,128,64,512]{3,2,1,0:T(8,128)S(1)} %get-tuple-element.3.results), custom_call_target="tpu_custom_call" | custom-call | tf_op jit(solution)/shard_map/write_results/pallas_call | solution.py:349
where the time goes:
time: 745 us
  Pallas kernels  744 us (100%)
    pallas_call x1, Pallas kernels, local_step(): pl.pallas_call(muon_kernel, name='muon_step', out_shape=(pltpu.VMEM((2, n...  733 us

commit v1 on v0

--- a/solution.py
+++ b/solution.py
@@ -25,7 +25,7 @@
 XSLOTS = 5
 HOLD = 2
 RSLOTS = 6
-PIECES = 4
+PIECES = 16
 MESH = pl.DeviceIdType.MESH
 
 
@@ -44,6 +44,8 @@
     partner = y * 4 + x * 2 + (1 - c)
     x_nbr = y * 4 + (1 - x) * 2
     y_nbr = (1 - y) * 4 + x * 2
+    diagonal = (1 - y) * 4 + (1 - x) * 2
+    peers = [base + core for base in (diagonal, x_nbr, y_nbr) for core in (c, 1 - c)] + [partner]
 
     def remote(src, dst, send, recv, dev):
         return pltpu.make_async_remote_copy(
@@ -51,8 +53,8 @@
             device_id={"data": dev}, device_id_type=MESH)
 
     barrier = pltpu.get_barrier_semaphore()
-    for r in range(1, NDEV):
-        pl.semaphore_signal(barrier, inc=1, device_id={"data": (me + r) % NDEV}, device_id_type=MESH)
+    for peer in peers:
+        pl.semaphore_signal(barrier, inc=1, device_id={"data": peer}, device_id_type=MESH)
     pl.semaphore_wait(barrier, NDEV - 1)
 
     def raw_copies(k):
@@ -94,18 +96,18 @@
         return pltpu.make_async_copy(w.at[rng], w_out.at[rng], w_in.at[k])
 
     def own_send(k, r):
-        j = (me + r) % NDEV
+        j = peers[r]
         slot = k % SLOTS
         return remote(stage.at[slot, j], owned.at[k % RSLOTS, pl.ds(me * rows, rows)],
                       own_s.at[slot, r], own_r.at[k, r], j)
 
     def nrm_send(k, r):
-        j = (me + r) % NDEV
+        j = peers[r]
         slot = k % SLOTS
         return remote(nstage.at[slot, j], owned_n.at[k, me], nrm_s.at[slot, r], nrm_r.at[k, r], j)
 
     def back_send(k, r):
-        j = (me + r) % NDEV
+        j = peers[r]
         slot = k % XSLOTS
         return remote(xbuf.at[slot, pl.ds(j * rows, rows)], xin.at[k % RSLOTS, me],
                       back_s.at[slot, r], back_r.at[k, r], j)
@@ -153,7 +155,7 @@
 
         @pl.when(k >= SLOTS)
         def _():
-            for r in range(1, NDEV):
+            for r in range(NDEV - 1):
                 own_send(k - SLOTS, r).wait_send()
                 nrm_send(k - SLOTS, r).wait_send()
 
@@ -165,7 +167,7 @@
             sq = jnp.sum(new * new, axis=0, keepdims=True)
             nstage[slot, j] = (sq[:, :128] + sq[:, 128:256]) + (sq[:, 256:384] + sq[:, 384:])
 
-        for r in range(1, NDEV):
+        for r in range(NDEV - 1):
             own_send(k, r).start()
             nrm_send(k, r).start()
         owned[k % RSLOTS, pl.ds(pl.multiple_of(me * rows, rows), rows)] = stage[slot, me]
@@ -180,10 +182,10 @@
 
         @pl.when(k >= XSLOTS)
         def _():
-            for r in range(1, NDEV):
+            for r in range(NDEV - 1):
                 back_send(k - XSLOTS, r).wait_send()
 
-        for r in range(1, NDEV):
+        for r in range(NDEV - 1):
             own_send(k, r).wait_recv()
             nrm_send(k, r).wait_recv()
         sq = jnp.sum(owned_n[k], axis=0)
@@ -209,17 +211,15 @@
         xin[k % RSLOTS, me] = xbuf[slot, pl.ds(pl.multiple_of(me * rows, rows), rows)]
 
     def send_back(k):
-        for r in range(1, NDEV):
+        for r in range(NDEV - 1):
             back_send(k, r).start()
 
     def update_weights(k):
         w_load(k).wait()
-        for r in range(1, NDEV):
-            j = (me + NDEV - r) % NDEV
-            pltpu.make_async_copy(xin.at[k % RSLOTS, j], xin.at[k % RSLOTS, j], back_r.at[k, r]).wait()
-
-        @pl.loop(0, CHUNK)
-        def _(j):
+        for r in range(-1, NDEV - 1):
+            j = me if r < 0 else peers[r]
+            if r >= 0:
+                pltpu.make_async_copy(xin.at[k % RSLOTS, j], xin.at[k % RSLOTS, j], back_r.at[k, r]).wait()
             old = w_out[k * CHUNK + j]
             step = xin[k % RSLOTS, j].astype(jnp.float32) * rms_scale
             w_out[k * CHUNK + j] = old - LEARN_RATE * (step + WEIGHT_DECAY * old)
@@ -265,10 +265,6 @@
     orthogonalize(last)
     send_back(last)
 
-    @pl.loop(steps - 4 - HOLD, steps)
-    def _(k):
-        update_weights(k)
-
     @pl.loop(0, steps)
     def _(k):
         for copy in raw_copies(k):
@@ -278,13 +274,17 @@
     def _(k):
         for s in range(2):
             part_copy(k, s).wait_send()
-        for r in range(1, NDEV):
+        for r in range(NDEV - 1):
             own_send(k, r).wait_send()
             nrm_send(k, r).wait_send()
 
+    @pl.loop(steps - 4 - HOLD, steps)
+    def _(k):
+        update_weights(k)
+
     @pl.loop(steps - XSLOTS, steps)
     def _(k):
-        for r in range(1, NDEV):
+        for r in range(NDEV - 1):
             back_send(k, r).wait_send()
 
 

time: 745 us -> 745 us (level)
  no operation moved by 1% of the time
where the time goes in v1:
time: 745 us
  Pallas kernels  744 us (100%)
    pallas_call x1, Pallas kernels, local_step(): pl.pallas_call(muon_kernel, name='muon_step', out_shape=(pltpu.VMEM((2, n...  733 us

profile of v1, /device:TPU:0, one launch (start us, length us, event | category | flops | bytes accessed | tf_op | source)
XLA Modules:
  0.0 745.0 jit_solution(15871334019537775625)
XLA Ops:
  0.6 733.2 %muon_step.1 = (f32[2,128,64,512]{3,2,1,0:T(8,128)S(1)}, bf16[16,2,3,4,2,64,512]{6,5,4,3,2,1,0:T(8,128)(2,1)}) custom-call(bf16[128,2,2,2,64,512]{5,4,3,2,1,0:T(8,128)(2,1)} %bitcast.grad, f32[128,64,512]{2,1,0:T(8,128)} %mom.1, f32[128,64,512]{2,1,0:T(8,128)} %w.1), custom_call_target="tpu_custom_call" | custom-call | tf_op jit(solution)/shard_map/muon_step/pallas_call | solution.py:317
  733.8 11.2 %write_results.1 = (f32[128,64,512]{2,1,0:T(8,128)}, f32[128,64,512]{2,1,0:T(8,128)}) custom-call(f32[2,128,64,512]{3,2,1,0:T(8,128)S(1)} %get-tuple-element.3.results), custom_call_target="tpu_custom_call" | custom-call | tf_op jit(solution)/shard_map/write_results/pallas_call | solution.py:349

commit v2 on v1

--- a/solution.py
+++ b/solution.py
@@ -20,6 +20,7 @@
 NDEV = 8
 CHUNK = 8
 HALF = 4
+PAIR = 2
 AHEAD = 2
 SLOTS = 3
 XSLOTS = 5
@@ -57,31 +58,27 @@
         pl.semaphore_signal(barrier, inc=1, device_id={"data": peer}, device_id_type=MESH)
     pl.semaphore_wait(barrier, NDEV - 1)
 
-    def raw_copies(k):
-        a = pl.ds(k * CHUNK, HALF)
-        b = pl.ds(k * CHUNK + HALF, HALF)
+    def raw_copies(q):
+        rng = pl.ds(q * PAIR, PAIR)
         out = []
         for dc in range(2):
-            out.append(remote(grad.at[a, :, 1 - x, dc], raw.at[k, 0, 1 + c],
-                              raw_s.at[k, 0, 1 + dc], raw_r.at[k, 0, 1 + c], x_nbr + dc))
-            out.append(remote(grad.at[b, 1 - y, :, dc], raw.at[k, 1, 1 + c],
-                              raw_s.at[k, 1, 1 + dc], raw_r.at[k, 1, 1 + c], y_nbr + dc))
-        out.append(remote(grad.at[a, :, x, 1 - c], raw.at[k, 0, 0], raw_s.at[k, 0, 0], raw_r.at[k, 0, 0], partner))
-        out.append(remote(grad.at[b, y, :, 1 - c], raw.at[k, 1, 0], raw_s.at[k, 1, 0], raw_r.at[k, 1, 0], partner))
+            out.append(remote(grad.at[rng, 0, :, :, 1 - x, dc], raw.at[q, 0, 1 + c],
+                              raw_s.at[q, 0, 1 + dc], raw_r.at[q, 0, 1 + c], x_nbr + dc))
+            out.append(remote(grad.at[rng, 1, :, 1 - y, :, dc], raw.at[q, 1, 1 + c],
+                              raw_s.at[q, 1, 1 + dc], raw_r.at[q, 1, 1 + c], y_nbr + dc))
+        out.append(remote(grad.at[rng, 0, :, :, x, 1 - c], raw.at[q, 0, 0], raw_s.at[q, 0, 0], raw_r.at[q, 0, 0], partner))
+        out.append(remote(grad.at[rng, 1, :, y, :, 1 - c], raw.at[q, 1, 0], raw_s.at[q, 1, 0], raw_r.at[q, 1, 0], partner))
         return out
 
-    def raw_arrival(k, s, i):
-        return pltpu.make_async_copy(raw.at[k, s, i], raw.at[k, s, i], raw_r.at[k, s, i])
+    def raw_arrival(q, s, i):
+        return pltpu.make_async_copy(raw.at[q, s, i], raw.at[q, s, i], raw_r.at[q, s, i])
 
     def own_copy(k, s):
-        if s == 0:
-            src = grad.at[pl.ds(k * CHUNK, HALF), :, x, c]
-        else:
-            src = grad.at[pl.ds(k * CHUNK + HALF, HALF), y, :, c]
+        src = grad.at[k, 0, :, :, x, c] if s == 0 else grad.at[k, 1, :, y, :, c]
         return pltpu.make_async_copy(src, inbuf.at[s, 0], in_sem.at[s, 0])
 
     def raw_load(k, s, i):
-        return pltpu.make_async_copy(raw.at[k, s, i], inbuf.at[s, 1 + i], in_sem.at[s, 1 + i])
+        return pltpu.make_async_copy(raw.at[k // PAIR, s, i, k % PAIR], inbuf.at[s, 1 + i], in_sem.at[s, 1 + i])
 
     def part_copy(k, s):
         slot = k % SLOTS
@@ -114,9 +111,14 @@
 
     def sum_chunk(k):
         slot = k % SLOTS
+        @pl.when(k % PAIR == 0)
+        def _():
+            for s in range(2):
+                for i in range(3):
+                    raw_arrival(k // PAIR, s, i).wait()
+
         for s in range(2):
             for i in range(3):
-                raw_arrival(k, s, i).wait()
                 raw_load(k, s, i).start()
 
         @pl.when(k >= SLOTS)
@@ -224,8 +226,8 @@
             step = xin[k % RSLOTS, j].astype(jnp.float32) * rms_scale
             w_out[k * CHUNK + j] = old - LEARN_RATE * (step + WEIGHT_DECAY * old)
 
-    for k in range(AHEAD):
-        for copy in raw_copies(k):
+    for q in range(AHEAD // PAIR):
+        for copy in raw_copies(q):
             copy.start()
     for s in range(2):
         own_copy(0, s).start()
@@ -233,9 +235,9 @@
 
     @pl.loop(0, steps)
     def _(t):
-        @pl.when(t + AHEAD < steps)
-        def _():
-            for copy in raw_copies(t + AHEAD):
+        @pl.when((t % PAIR == 0) & (t + AHEAD < steps))
+        def _():
+            for copy in raw_copies((t + AHEAD) // PAIR):
                 copy.start()
 
         sum_chunk(t)
@@ -265,9 +267,9 @@
     orthogonalize(last)
     send_back(last)
 
-    @pl.loop(0, steps)
-    def _(k):
-        for copy in raw_copies(k):
+    @pl.loop(0, steps // PAIR)
+    def _(q):
+        for copy in raw_copies(q):
             copy.wait_send()
 
     @pl.loop(steps - SLOTS, steps)
@@ -309,7 +311,7 @@
         n_mats, rows, n_cols = w_rows.shape
         n_rows = rows * NDEV
         steps = n_mats // CHUNK
-        grad_view = grad_full.reshape(n_mats, 2, 2, 2, rows, n_cols)
+        grad_view = grad_full.reshape(steps, 2, HALF, 2, 2, 2, rows, n_cols)
         f32, bf16 = jnp.float32, jnp.bfloat16
         dma = pltpu.SemaphoreType.DMA
         hbm = pl.BlockSpec(memory_space=pltpu.HBM)
@@ -319,7 +321,7 @@
             name="muon_step",
             out_shape=(
                 pltpu.VMEM((2, n_mats, rows, n_cols), f32),
-                jax.ShapeDtypeStruct((steps, 2, 3, HALF, 2, rows, n_cols), bf16),
+                jax.ShapeDtypeStruct((steps // PAIR, 2, 3, PAIR, HALF, 2, rows, n_cols), bf16),
             ),
             in_specs=[hbm] * 3,
             out_specs=(vmem, hbm),
@@ -336,7 +338,7 @@
                 pltpu.VMEM((RSLOTS, CHUNK, rows, n_cols), bf16),
                 pltpu.VMEM((n_rows, n_rows), bf16),
                 pltpu.VMEM((n_rows, n_rows), bf16),
-                dma((steps, 2, 3)), dma((steps, 2, 3)),
+                dma((steps // PAIR, 2, 3)), dma((steps // PAIR, 2, 3)),
                 dma((SLOTS, 2)), dma((steps, 2)),
                 dma((SLOTS, NDEV)), dma((steps, NDEV)),
                 dma((SLOTS, NDEV)), dma((steps, NDEV)),

time: 745 us -> 744 us (level)
  no operation moved by 1% of the time
where the time goes in v2:
time: 744 us
  Pallas kernels  743 us (100%)
    pallas_call x1, Pallas kernels, local_step(): pl.pallas_call(muon_kernel, name='muon_step', out_shape=(pltpu.VMEM((2, n...  732 us

profile of v2, /device:TPU:0, one launch (start us, length us, event | category | flops | bytes accessed | tf_op | source)
XLA Modules:
  0.0 744.1 jit_solution(12601856419033596598)
XLA Ops:
  0.6 732.3 %muon_step.1 = (f32[2,128,64,512]{3,2,1,0:T(8,128)S(1)}, bf16[8,2,3,2,4,2,64,512]{7,6,5,4,3,2,1,0:T(8,128)(2,1)}) custom-call(bf16[16,2,4,2,2,2,64,512]{7,6,5,4,3,2,1,0:T(8,128)(2,1)} %bitcast.grad, f32[128,64,512]{2,1,0:T(8,128)} %mom.1, f32[128,64,512]{2,1,0:T(8,128)} %w.1), custom_call_target="tpu_custom_call" | custom-call | tf_op jit(solution)/shard_map/muon_step/pallas_call | solution.py:319
  733.0 11.2 %write_results.1 = (f32[128,64,512]{2,1,0:T(8,128)}, f32[128,64,512]{2,1,0:T(8,128)}) custom-call(f32[2,128,64,512]{3,2,1,0:T(8,128)S(1)} %get-tuple-element.3.results), custom_call_target="tpu_custom_call" | custom-call | tf_op jit(solution)/shard_map/write_results/pallas_call | solution.py:351

commit v3 on v2

--- a/solution.py
+++ b/solution.py
@@ -23,9 +23,12 @@
 PAIR = 2
 AHEAD = 2
 SLOTS = 3
-XSLOTS = 5
+GROUP = 2
+GSLOTS = 2
+OSLOTS = 2
+XSLOTS = 3
+RSLOTS = 3
 HOLD = 2
-RSLOTS = 6
 PIECES = 16
 MESH = pl.DeviceIdType.MESH
 
@@ -92,22 +95,19 @@
         rng = pl.ds(k * CHUNK, CHUNK)
         return pltpu.make_async_copy(w.at[rng], w_out.at[rng], w_in.at[k])
 
-    def own_send(k, r):
-        j = peers[r]
-        slot = k % SLOTS
-        return remote(stage.at[slot, j], owned.at[k % RSLOTS, pl.ds(me * rows, rows)],
-                      own_s.at[slot, r], own_r.at[k, r], j)
-
-    def nrm_send(k, r):
-        j = peers[r]
-        slot = k % SLOTS
-        return remote(nstage.at[slot, j], owned_n.at[k, me], nrm_s.at[slot, r], nrm_r.at[k, r], j)
-
-    def back_send(k, r):
-        j = peers[r]
-        slot = k % XSLOTS
-        return remote(xbuf.at[slot, pl.ds(j * rows, rows)], xin.at[k % RSLOTS, me],
-                      back_s.at[slot, r], back_r.at[k, r], j)
+    def own_send(g, r):
+        slot = g % GSLOTS
+        return remote(stage.at[slot, peers[r]], owned.at[g % OSLOTS, :, pl.ds(me * rows, rows)],
+                      own_s.at[slot, r], own_r.at[g, r], peers[r])
+
+    def nrm_send(g, r):
+        slot = g % GSLOTS
+        return remote(nstage.at[slot, peers[r]], owned_n.at[g, me], nrm_s.at[slot, r], nrm_r.at[g, r], peers[r])
+
+    def back_send(g, r):
+        slot = g % XSLOTS
+        return remote(xbuf.at[slot, :, pl.ds(peers[r] * rows, rows)], xin.at[g % RSLOTS, me],
+                      back_s.at[slot, r], back_r.at[g, r], peers[r])
 
     def sum_chunk(k):
         slot = k % SLOTS
@@ -151,80 +151,94 @@
 
     def finish_chunk(k):
         slot = k % SLOTS
+        g, i = k // GROUP, k % GROUP
+        gslot = g % GSLOTS
         mom_load(k).wait()
         for s in range(2):
             part_copy(k, s).wait_recv()
 
-        @pl.when(k >= SLOTS)
+        @pl.when((i == 0) & (g >= GSLOTS))
         def _():
             for r in range(NDEV - 1):
-                own_send(k - SLOTS, r).wait_send()
-                nrm_send(k - SLOTS, r).wait_send()
+                own_send(g - GSLOTS, r).wait_send()
+                nrm_send(g - GSLOTS, r).wait_send()
 
         @pl.loop(0, CHUNK)
         def _(j):
             new = MOMENTUM_COEF * momb[slot, j] + (kept[k % 2, j] + mom_out[k * CHUNK + j])
             mom_out[k * CHUNK + j] = new
-            stage[slot, j] = new.astype(jnp.bfloat16)
+            stage[gslot, j, i] = new.astype(jnp.bfloat16)
             sq = jnp.sum(new * new, axis=0, keepdims=True)
-            nstage[slot, j] = (sq[:, :128] + sq[:, 128:256]) + (sq[:, 256:384] + sq[:, 384:])
+            nstage[gslot, j, i] = (sq[:, :128] + sq[:, 128:256]) + (sq[:, 256:384] + sq[:, 384:])
+
+        @pl.when(i == GROUP - 1)
+        def _():
+            for r in range(NDEV - 1):
+                own_send(g, r).start()
+                nrm_send(g, r).start()
+
+        owned[g % OSLOTS, i, pl.ds(pl.multiple_of(me * rows, rows), rows)] = stage[gslot, me, i]
+        owned_n[g, me, i] = nstage[gslot, me, i]
+
+        @pl.when(k + 1 < steps)
+        def _():
+            mom_load(k + 1).start()
+
+    def orthogonalize(g):
+        slot = g % XSLOTS
+
+        @pl.when(g >= XSLOTS)
+        def _():
+            for r in range(NDEV - 1):
+                back_send(g - XSLOTS, r).wait_send()
 
         for r in range(NDEV - 1):
-            own_send(k, r).start()
-            nrm_send(k, r).start()
-        owned[k % RSLOTS, pl.ds(pl.multiple_of(me * rows, rows), rows)] = stage[slot, me]
-        owned_n[k, me] = nstage[slot, me]
-
-        @pl.when(k + 1 < steps)
-        def _():
-            mom_load(k + 1).start()
-
-    def orthogonalize(k):
-        slot = k % XSLOTS
-
-        @pl.when(k >= XSLOTS)
-        def _():
-            for r in range(NDEV - 1):
-                back_send(k - XSLOTS, r).wait_send()
-
+            own_send(g, r).wait_recv()
+            nrm_send(g, r).wait_recv()
+
+        @pl.loop(0, GROUP)
+        def _(i):
+            sq = owned_n[g, 0, i]
+            for j in range(1, NDEV):
+                sq = sq + owned_n[g, j, i]
+            den = jnp.sqrt(jnp.sum(sq, axis=1, keepdims=True)) + NORM_EPS
+
+            @pl.loop(0, NDEV)
+            def _(j):
+                blk = pl.ds(pl.multiple_of(j * rows, rows), rows)
+                xbuf[slot, i, blk] = (owned[g % OSLOTS, i, blk].astype(jnp.float32) / den).astype(jnp.bfloat16)
+
+            @pl.loop(0, NS_ITERS)
+            def _(_):
+                cur = xbuf[slot, i]
+                gram[...] = lax.dot_general(cur, cur, (((1,), (1,)), ((), ())),
+                                            preferred_element_type=jnp.float32).astype(jnp.bfloat16)
+                gm = gram[...]
+                sqr = jnp.dot(gm, gm, preferred_element_type=jnp.float32)
+                poly[...] = (COEF_B * gm.astype(jnp.float32) + COEF_C * sqr).astype(jnp.bfloat16)
+                px = jnp.dot(poly[...], cur, preferred_element_type=jnp.float32)
+                xbuf[slot, i] = (COEF_A * cur.astype(jnp.float32) + px).astype(jnp.bfloat16)
+
+            xin[g % RSLOTS, me, i] = xbuf[slot, i, pl.ds(pl.multiple_of(me * rows, rows), rows)]
+
+    def send_back(g):
         for r in range(NDEV - 1):
-            own_send(k, r).wait_recv()
-            nrm_send(k, r).wait_recv()
-        sq = jnp.sum(owned_n[k], axis=0)
-        nrm = jnp.sqrt(jnp.sum(sq, axis=1, keepdims=True))
-        den = nrm + NORM_EPS
-
-        @pl.loop(0, NDEV)
-        def _(i):
-            blk = pl.ds(pl.multiple_of(i * rows, rows), rows)
-            xbuf[slot, blk] = (owned[k % RSLOTS, blk].astype(jnp.float32) / den).astype(jnp.bfloat16)
-
-        @pl.loop(0, NS_ITERS)
-        def _(_):
-            cur = xbuf[slot]
-            gram[...] = lax.dot_general(cur, cur, (((1,), (1,)), ((), ())),
-                                        preferred_element_type=jnp.float32).astype(jnp.bfloat16)
-            g = gram[...]
-            sqr = jnp.dot(g, g, preferred_element_type=jnp.float32)
-            poly[...] = (COEF_B * g.astype(jnp.float32) + COEF_C * sqr).astype(jnp.bfloat16)
-            px = jnp.dot(poly[...], cur, preferred_element_type=jnp.float32)
-            xbuf[slot] = (COEF_A * cur.astype(jnp.float32) + px).astype(jnp.bfloat16)
-
-        xin[k % RSLOTS, me] = xbuf[slot, pl.ds(pl.multiple_of(me * rows, rows), rows)]
-
-    def send_back(k):
-        for r in range(NDEV - 1):
-            back_send(k, r).start()
-
-    def update_weights(k):
-        w_load(k).wait()
+            back_send(g, r).start()
+
+    def update_weights(g):
+        for i in range(GROUP):
+            w_load(g * GROUP + i).wait()
         for r in range(-1, NDEV - 1):
             j = me if r < 0 else peers[r]
             if r >= 0:
-                pltpu.make_async_copy(xin.at[k % RSLOTS, j], xin.at[k % RSLOTS, j], back_r.at[k, r]).wait()
-            old = w_out[k * CHUNK + j]
-            step = xin[k % RSLOTS, j].astype(jnp.float32) * rms_scale
-            w_out[k * CHUNK + j] = old - LEARN_RATE * (step + WEIGHT_DECAY * old)
+                pltpu.make_async_copy(xin.at[g % RSLOTS, j], xin.at[g % RSLOTS, j], back_r.at[g, r]).wait()
+
+            @pl.loop(0, GROUP)
+            def _(i):
+                m = (g * GROUP + i) * CHUNK + j
+                old = w_out[m]
+                step = xin[g % RSLOTS, j, i].astype(jnp.float32) * rms_scale
+                w_out[m] = old - LEARN_RATE * (step + WEIGHT_DECAY * old)
 
     for q in range(AHEAD // PAIR):
         for copy in raw_copies(q):
@@ -242,30 +256,25 @@
 
         sum_chunk(t)
 
-        @pl.when(t >= 2 + HOLD)
-        def _():
-            send_back(t - 2 - HOLD)
+        def at(lag, work):
+            @pl.when(((t - lag) % GROUP == 0) & (t >= lag + GROUP))
+            def _():
+                work((t - lag) // GROUP - 1)
+
+        at(1 + HOLD, send_back)
 
         @pl.when(t >= 1)
         def _():
             finish_chunk(t - 1)
 
-        @pl.when(t >= 2)
-        def _():
-            orthogonalize(t - 2)
-
-        @pl.when(t >= 4 + HOLD)
-        def _():
-            update_weights(t - 4 - HOLD)
-
-    last = steps - 1
-    send_back(last - 3)
-    finish_chunk(last)
-    send_back(last - 2)
-    orthogonalize(last - 1)
-    send_back(last - 1)
-    orthogonalize(last)
-    send_back(last)
+        at(1, orthogonalize)
+        at(3 + HOLD, update_weights)
+
+    groups = steps // GROUP
+    finish_chunk(steps - 1)
+    send_back(groups - 2)
+    orthogonalize(groups - 1)
+    send_back(groups - 1)
 
     @pl.loop(0, steps // PAIR)
     def _(q):
@@ -276,18 +285,21 @@
     def _(k):
         for s in range(2):
             part_copy(k, s).wait_send()
+
+    @pl.loop(groups - GSLOTS, groups)
+    def _(g):
         for r in range(NDEV - 1):
-            own_send(k, r).wait_send()
-            nrm_send(k, r).wait_send()
-
-    @pl.loop(steps - 4 - HOLD, steps)
-    def _(k):
-        update_weights(k)
-
-    @pl.loop(steps - XSLOTS, steps)
-    def _(k):
+            own_send(g, r).wait_send()
+            nrm_send(g, r).wait_send()
+
+    @pl.loop((steps - 1 - 3 - HOLD) // GROUP, groups)
+    def _(g):
+        update_weights(g)
+
+    @pl.loop(groups - XSLOTS, groups)
+    def _(g):
         for r in range(NDEV - 1):
-            back_send(k, r).wait_send()
+            back_send(g, r).wait_send()
 
 
 def write_kernel(results, w_out, mom_out, sems):
@@ -311,6 +323,7 @@
         n_mats, rows, n_cols = w_rows.shape
         n_rows = rows * NDEV
         steps = n_mats // CHUNK
+        groups = steps // GROUP
         grad_view = grad_full.reshape(steps, 2, HALF, 2, 2, 2, rows, n_cols)
         f32, bf16 = jnp.float32, jnp.bfloat16
         dma = pltpu.SemaphoreType.DMA
@@ -330,19 +343,19 @@
                 pltpu.VMEM((2, CHUNK, rows, n_cols), f32),
                 pltpu.VMEM((SLOTS, 2, HALF, rows, n_cols), f32),
                 pltpu.VMEM((SLOTS, CHUNK, rows, n_cols), f32),
-                pltpu.VMEM((SLOTS, CHUNK, rows, n_cols), bf16),
-                pltpu.VMEM((RSLOTS, n_rows, n_cols), bf16),
-                pltpu.VMEM((SLOTS, CHUNK, 1, 128), f32),
-                pltpu.VMEM((steps, NDEV, 1, 128), f32),
-                pltpu.VMEM((XSLOTS, n_rows, n_cols), bf16),
-                pltpu.VMEM((RSLOTS, CHUNK, rows, n_cols), bf16),
+                pltpu.VMEM((GSLOTS, NDEV, GROUP, rows, n_cols), bf16),
+                pltpu.VMEM((OSLOTS, GROUP, n_rows, n_cols), bf16),
+                pltpu.VMEM((GSLOTS, NDEV, GROUP, 1, 128), f32),
+                pltpu.VMEM((groups, NDEV, GROUP, 1, 128), f32),
+                pltpu.VMEM((XSLOTS, GROUP, n_rows, n_cols), bf16),
+                pltpu.VMEM((RSLOTS, NDEV, GROUP, rows, n_cols), bf16),
                 pltpu.VMEM((n_rows, n_rows), bf16),
                 pltpu.VMEM((n_rows, n_rows), bf16),
                 dma((steps // PAIR, 2, 3)), dma((steps // PAIR, 2, 3)),
                 dma((SLOTS, 2)), dma((steps, 2)),
-                dma((SLOTS, NDEV)), dma((steps, NDEV)),
-                dma((SLOTS, NDEV)), dma((steps, NDEV)),
-                dma((XSLOTS, NDEV)), dma((steps, NDEV)),
+                dma((GSLOTS, NDEV)), dma((groups, NDEV)),
+                dma((GSLOTS, NDEV)), dma((groups, NDEV)),
+                dma((XSLOTS, NDEV)), dma((groups, NDEV)),
                 dma((2, 4)), dma((SLOTS,)), dma((steps,)),
             ],
             compiler_params=pltpu.CompilerParams(

time: 744 us -> 746 us (level)
  no operation moved by 1% of the time
where the time goes in v3:
time: 746 us; the launch traced here: 745 us
  Pallas kernels  745 us (100%)
    pallas_call x1, Pallas kernels, local_step(): pl.pallas_call(muon_kernel, name='muon_step', out_shape=(pltpu.VMEM((2, n...  734 us

profile of v3, /device:TPU:0, one launch (start us, length us, event | category | flops | bytes accessed | tf_op | source)
XLA Modules:
  0.0 745.4 jit_solution(17828865996746412517)
XLA Ops:
  0.6 733.6 %muon_step.1 = (f32[2,128,64,512]{3,2,1,0:T(8,128)S(1)}, bf16[8,2,3,2,4,2,64,512]{7,6,5,4,3,2,1,0:T(8,128)(2,1)}) custom-call(bf16[16,2,4,2,2,2,64,512]{7,6,5,4,3,2,1,0:T(8,128)(2,1)} %bitcast.grad, f32[128,64,512]{2,1,0:T(8,128)} %mom.1, f32[128,64,512]{2,1,0:T(8,128)} %w.1), custom_call_target="tpu_custom_call" | custom-call | tf_op jit(solution)/shard_map/muon_step/pallas_call | solution.py:332
  734.3 11.2 %write_results.1 = (f32[128,64,512]{2,1,0:T(8,128)}, f32[128,64,512]{2,1,0:T(8,128)}) custom-call(f32[2,128,64,512]{3,2,1,0:T(8,128)S(1)} %get-tuple-element.3.results), custom_call_target="tpu_custom_call" | custom-call | tf_op jit(solution)/shard_map/write_results/pallas_call | solution.py:364

commit v4 on v3

--- a/solution.py
+++ b/solution.py
@@ -23,12 +23,12 @@
 PAIR = 2
 AHEAD = 2
 SLOTS = 3
-GROUP = 2
+GROUP = 4
 GSLOTS = 2
 OSLOTS = 2
-XSLOTS = 3
-RSLOTS = 3
-HOLD = 2
+XSLOTS = 2
+RSLOTS = 2
+HOLD = 3
 PIECES = 16
 MESH = pl.DeviceIdType.MESH
 
@@ -36,7 +36,7 @@
 def muon_kernel(
     grad, mom, w, results, raw,
     inbuf, kept, part, momb, stage, owned, nstage, owned_n, xbuf, xin, gram, poly,
-    raw_s, raw_r, part_s, part_r, own_s, own_r, nrm_s, nrm_r, back_s, back_r,
+    raw_s, raw_r, part_s, part_r, own_s, own_r, nrm_s, nrm_r, back_s, back_r, tail_s, tail_r,
     in_sem, mom_in, w_in,
 ):
     n_mats, rows, cols = mom.shape
@@ -109,6 +109,11 @@
         return remote(xbuf.at[slot, :, pl.ds(peers[r] * rows, rows)], xin.at[g % RSLOTS, me],
                       back_s.at[slot, r], back_r.at[g, r], peers[r])
 
+    def tail_send(g, i, r):
+        slot = g % XSLOTS
+        return remote(xbuf.at[slot, i, pl.ds(peers[r] * rows, rows)], xin.at[g % RSLOTS, me, i],
+                      tail_s.at[i, r], tail_r.at[i, r], peers[r])
+
     def sum_chunk(k):
         slot = k % SLOTS
         @pl.when(k % PAIR == 0)
@@ -184,7 +189,7 @@
         def _():
             mom_load(k + 1).start()
 
-    def orthogonalize(g):
+    def orthogonalize(g, after=lambda i: None):
         slot = g % XSLOTS
 
         @pl.when(g >= XSLOTS)
@@ -219,26 +224,40 @@
                 px = jnp.dot(poly[...], cur, preferred_element_type=jnp.float32)
                 xbuf[slot, i] = (COEF_A * cur.astype(jnp.float32) + px).astype(jnp.bfloat16)
 
+            after(i)
             xin[g % RSLOTS, me, i] = xbuf[slot, i, pl.ds(pl.multiple_of(me * rows, rows), rows)]
 
-    def send_back(g):
-        for r in range(NDEV - 1):
+    def send_back(g, part=range(NDEV - 1)):
+        for r in part:
             back_send(g, r).start()
+
+    def update_rows(g, i, j):
+        m = (g * GROUP + i) * CHUNK + j
+        old = w_out[m]
+        step = xin[g % RSLOTS, j, i].astype(jnp.float32) * rms_scale
+        w_out[m] = old - LEARN_RATE * (step + WEIGHT_DECAY * old)
 
     def update_weights(g):
         for i in range(GROUP):
             w_load(g * GROUP + i).wait()
-        for r in range(-1, NDEV - 1):
-            j = me if r < 0 else peers[r]
-            if r >= 0:
+        for r in range(NDEV):
+            j = peers[r] if r < NDEV - 1 else me
+            if r < NDEV - 1:
                 pltpu.make_async_copy(xin.at[g % RSLOTS, j], xin.at[g % RSLOTS, j], back_r.at[g, r]).wait()
 
             @pl.loop(0, GROUP)
             def _(i):
-                m = (g * GROUP + i) * CHUNK + j
-                old = w_out[m]
-                step = xin[g % RSLOTS, j, i].astype(jnp.float32) * rms_scale
-                w_out[m] = old - LEARN_RATE * (step + WEIGHT_DECAY * old)
+                update_rows(g, i, j)
+
+    def update_last(g):
+        @pl.loop(0, GROUP)
+        def _(i):
+            w_load(g * GROUP + i).wait()
+            update_rows(g, i, me)
+            for r in range(NDEV - 1):
+                pltpu.make_async_copy(xin.at[g % RSLOTS, peers[r], i], xin.at[g % RSLOTS, peers[r], i],
+                                      tail_r.at[i, r]).wait()
+                update_rows(g, i, peers[r])
 
     for q in range(AHEAD // PAIR):
         for copy in raw_copies(q):
@@ -271,10 +290,17 @@
         at(3 + HOLD, update_weights)
 
     groups = steps // GROUP
+    last = groups - 1
+
+    def send_rows(i):
+        for r in range(NDEV - 1):
+            tail_send(last, i, r).start()
+
+    if GROUP > 2:
+        send_back(last - 1, range(0, NDEV - 1, 2))
     finish_chunk(steps - 1)
-    send_back(groups - 2)
-    orthogonalize(groups - 1)
-    send_back(groups - 1)
+    send_back(last - 1, range(1, NDEV - 1, 2) if GROUP > 2 else range(NDEV - 1))
+    orthogonalize(last, send_rows)
 
     @pl.loop(0, steps // PAIR)
     def _(q):
@@ -292,14 +318,17 @@
             own_send(g, r).wait_send()
             nrm_send(g, r).wait_send()
 
-    @pl.loop((steps - 1 - 3 - HOLD) // GROUP, groups)
+    @pl.loop((steps - 1 - 3 - HOLD) // GROUP, last)
     def _(g):
         update_weights(g)
 
-    @pl.loop(groups - XSLOTS, groups)
-    def _(g):
-        for r in range(NDEV - 1):
+    update_last(last)
+
+    for r in range(NDEV - 1):
+        for g in range(groups - XSLOTS, last):
             back_send(g, r).wait_send()
+        for i in range(GROUP):
+            tail_send(last, i, r).wait_send()
 
 
 def write_kernel(results, w_out, mom_out, sems):
@@ -356,6 +385,7 @@
                 dma((GSLOTS, NDEV)), dma((groups, NDEV)),
                 dma((GSLOTS, NDEV)), dma((groups, NDEV)),
                 dma((XSLOTS, NDEV)), dma((groups, NDEV)),
+                dma((GROUP, NDEV)), dma((GROUP, NDEV)),
                 dma((2, 4)), dma((SLOTS,)), dma((steps,)),
             ],
             compiler_params=pltpu.CompilerParams(

time: 746 us -> 784 us (1.051)
  Pallas kernels: 745 us -> 783 us
    pallas_call x1, Pallas kernels: 734 us -> 771 us  [local_step(): pl.pallas_call(muon_kernel, name='muon_step', out_shape=(pltpu.VMEM((2, n...]
where the time goes in v4:
time: 784 us; the launch traced here: 783 us
  Pallas kernels  783 us (100%)
    pallas_call x1, Pallas kernels, local_step(): pl.pallas_call(muon_kernel, name='muon_step', out_shape=(pltpu.VMEM((2, n...  771 us

profile of v4, /device:TPU:0, one launch (start us, length us, event | category | flops | bytes accessed | tf_op | source)
XLA Modules:
  0.0 783.2 jit_solution(18016266727025488550)
XLA Ops:
  0.6 771.5 %muon_step.1 = (f32[2,128,64,512]{3,2,1,0:T(8,128)S(1)}, bf16[8,2,3,2,4,2,64,512]{7,6,5,4,3,2,1,0:T(8,128)(2,1)}) custom-call(bf16[16,2,4,2,2,2,64,512]{7,6,5,4,3,2,1,0:T(8,128)(2,1)} %bitcast.grad, f32[128,64,512]{2,1,0:T(8,128)} %mom.1, f32[128,64,512]{2,1,0:T(8,128)} %w.1), custom_call_target="tpu_custom_call" | custom-call | tf_op jit(solution)/shard_map/muon_step/pallas_call | solution.py:361
  772.1 11.2 %write_results.1 = (f32[128,64,512]{2,1,0:T(8,128)}, f32[128,64,512]{2,1,0:T(8,128)}) custom-call(f32[2,128,64,512]{3,2,1,0:T(8,128)S(1)} %get-tuple-element.3.results), custom_call_target="tpu_custom_call" | custom-call | tf_op jit(solution)/shard_map/write_results/pallas_call | solution.py:394

commit v5 on v4

--- a/solution.py
+++ b/solution.py
@@ -23,12 +23,11 @@
 PAIR = 2
 AHEAD = 2
 SLOTS = 3
-GROUP = 4
+GROUP = 2
 GSLOTS = 2
-OSLOTS = 2
-XSLOTS = 2
-RSLOTS = 2
-HOLD = 3
+OSLOTS = 3
+XSLOTS = 3
+RSLOTS = 3
 PIECES = 16
 MESH = pl.DeviceIdType.MESH
 
@@ -189,9 +188,7 @@
         def _():
             mom_load(k + 1).start()
 
-    def orthogonalize(g, after=lambda i: None):
-        slot = g % XSLOTS
-
+    def owned_arrival(g):
         @pl.when(g >= XSLOTS)
         def _():
             for r in range(NDEV - 1):
@@ -201,34 +198,33 @@
             own_send(g, r).wait_recv()
             nrm_send(g, r).wait_recv()
 
-        @pl.loop(0, GROUP)
-        def _(i):
-            sq = owned_n[g, 0, i]
-            for j in range(1, NDEV):
-                sq = sq + owned_n[g, j, i]
-            den = jnp.sqrt(jnp.sum(sq, axis=1, keepdims=True)) + NORM_EPS
-
-            @pl.loop(0, NDEV)
-            def _(j):
-                blk = pl.ds(pl.multiple_of(j * rows, rows), rows)
-                xbuf[slot, i, blk] = (owned[g % OSLOTS, i, blk].astype(jnp.float32) / den).astype(jnp.bfloat16)
-
-            @pl.loop(0, NS_ITERS)
-            def _(_):
-                cur = xbuf[slot, i]
-                gram[...] = lax.dot_general(cur, cur, (((1,), (1,)), ((), ())),
-                                            preferred_element_type=jnp.float32).astype(jnp.bfloat16)
-                gm = gram[...]
-                sqr = jnp.dot(gm, gm, preferred_element_type=jnp.float32)
-                poly[...] = (COEF_B * gm.astype(jnp.float32) + COEF_C * sqr).astype(jnp.bfloat16)
-                px = jnp.dot(poly[...], cur, preferred_element_type=jnp.float32)
-                xbuf[slot, i] = (COEF_A * cur.astype(jnp.float32) + px).astype(jnp.bfloat16)
-
-            after(i)
-            xin[g % RSLOTS, me, i] = xbuf[slot, i, pl.ds(pl.multiple_of(me * rows, rows), rows)]
-
-    def send_back(g, part=range(NDEV - 1)):
-        for r in part:
+    def orthogonalize(g, i):
+        slot = g % XSLOTS
+        sq = owned_n[g, 0, i]
+        for j in range(1, NDEV):
+            sq = sq + owned_n[g, j, i]
+        den = jnp.sqrt(jnp.sum(sq, axis=1, keepdims=True)) + NORM_EPS
+
+        @pl.loop(0, NDEV)
+        def _(j):
+            blk = pl.ds(pl.multiple_of(j * rows, rows), rows)
+            xbuf[slot, i, blk] = (owned[g % OSLOTS, i, blk].astype(jnp.float32) / den).astype(jnp.bfloat16)
+
+        @pl.loop(0, NS_ITERS)
+        def _(_):
+            cur = xbuf[slot, i]
+            gram[...] = lax.dot_general(cur, cur, (((1,), (1,)), ((), ())),
+                                        preferred_element_type=jnp.float32).astype(jnp.bfloat16)
+            gm = gram[...]
+            sqr = jnp.dot(gm, gm, preferred_element_type=jnp.float32)
+            poly[...] = (COEF_B * gm.astype(jnp.float32) + COEF_C * sqr).astype(jnp.bfloat16)
+            px = jnp.dot(poly[...], cur, preferred_element_type=jnp.float32)
+            xbuf[slot, i] = (COEF_A * cur.astype(jnp.float32) + px).astype(jnp.bfloat16)
+
+        xin[g % RSLOTS, me, i] = xbuf[slot, i, pl.ds(pl.multiple_of(me * rows, rows), rows)]
+
+    def send_back(g):
+        for r in range(NDEV - 1):
             back_send(g, r).start()
 
     def update_rows(g, i, j):
@@ -280,27 +276,37 @@
             def _():
                 work((t - lag) // GROUP - 1)
 
-        at(1 + HOLD, send_back)
+        at(1 + GROUP, send_back)
 
         @pl.when(t >= 1)
         def _():
             finish_chunk(t - 1)
 
-        at(1, orthogonalize)
-        at(3 + HOLD, update_weights)
+        at(1, owned_arrival)
+
+        @pl.when(t >= 1 + GROUP)
+        def _():
+            orthogonalize((t - 1) // GROUP - 1, (t - 1) % GROUP)
+
+        at(3 + GROUP, update_weights)
 
     groups = steps // GROUP
     last = groups - 1
-
-    def send_rows(i):
-        for r in range(NDEV - 1):
-            tail_send(last, i, r).start()
-
-    if GROUP > 2:
-        send_back(last - 1, range(0, NDEV - 1, 2))
     finish_chunk(steps - 1)
-    send_back(last - 1, range(1, NDEV - 1, 2) if GROUP > 2 else range(NDEV - 1))
-    orthogonalize(last, send_rows)
+
+    @pl.loop(GROUP - 1, 2 * GROUP)
+    def _(n):
+        @pl.when(n == GROUP)
+        def _():
+            send_back(last - 1)
+            owned_arrival(last)
+
+        orthogonalize(last - 1 + n // GROUP, n % GROUP)
+
+        @pl.when(n >= GROUP)
+        def _():
+            for r in range(NDEV - 1):
+                tail_send(last, n - GROUP, r).start()
 
     @pl.loop(0, steps // PAIR)
     def _(q):
@@ -318,7 +324,7 @@
             own_send(g, r).wait_send()
             nrm_send(g, r).wait_send()
 
-    @pl.loop((steps - 1 - 3 - HOLD) // GROUP, last)
+    @pl.loop((steps - 4 - GROUP) // GROUP, last)
     def _(g):
         update_weights(g)
 

time: 784 us -> 742 us (0.946)
  Pallas kernels: 783 us -> 741 us
    pallas_call x1, Pallas kernels: 771 us -> 730 us  [local_step(): pl.pallas_call(muon_kernel, name='muon_step', out_shape=(pltpu.VMEM((2, n...]
where the time goes in v5:
time: 742 us
  Pallas kernels  741 us (100%)
    pallas_call x1, Pallas kernels, local_step(): pl.pallas_call(muon_kernel, name='muon_step', out_shape=(pltpu.VMEM((2, n...  730 us

profile of v5, /device:TPU:0, one launch (start us, length us, event | category | flops | bytes accessed | tf_op | source)
XLA Modules:
  0.0 741.6 jit_solution(16921868765505675906)
XLA Ops:
  0.6 729.9 %muon_step.1 = (f32[2,128,64,512]{3,2,1,0:T(8,128)S(1)}, bf16[8,2,3,2,4,2,64,512]{7,6,5,4,3,2,1,0:T(8,128)(2,1)}) custom-call(bf16[16,2,4,2,2,2,64,512]{7,6,5,4,3,2,1,0:T(8,128)(2,1)} %bitcast.grad, f32[128,64,512]{2,1,0:T(8,128)} %mom.1, f32[128,64,512]{2,1,0:T(8,128)} %w.1), custom_call_target="tpu_custom_call" | custom-call | tf_op jit(solution)/shard_map/muon_step/pallas_call | solution.py:367
  730.5 11.2 %write_results.1 = (f32[128,64,512]{2,1,0:T(8,128)}, f32[128,64,512]{2,1,0:T(8,128)}) custom-call(f32[2,128,64,512]{3,2,1,0:T(8,128)S(1)} %get-tuple-element.3.results), custom_call_target="tpu_custom_call" | custom-call | tf_op jit(solution)/shard_map/write_results/pallas_call | solution.py:400

commit v6 on v5

--- a/solution.py
+++ b/solution.py
@@ -28,14 +28,14 @@
 OSLOTS = 3
 XSLOTS = 3
 RSLOTS = 3
-PIECES = 16
+PIECES = 4
 MESH = pl.DeviceIdType.MESH
 
 
 def muon_kernel(
     grad, mom, w, results, raw,
-    inbuf, kept, part, momb, stage, owned, nstage, owned_n, xbuf, xin, gram, poly,
-    raw_s, raw_r, part_s, part_r, own_s, own_r, nrm_s, nrm_r, back_s, back_r, tail_s, tail_r,
+    inbuf, kept, part, momb, stage, swap, owned, nstage, nswap, owned_n, xbuf, xin, gram, poly,
+    raw_s, raw_r, part_s, part_r, swap_s, swap_r, own_s, own_r, nrm_s, nrm_r, back_s, back_r, tail_s, tail_r,
     in_sem, mom_in, w_in,
 ):
     n_mats, rows, cols = mom.shape
@@ -50,6 +50,9 @@
     diagonal = (1 - y) * 4 + (1 - x) * 2
     peers = [base + core for base in (diagonal, x_nbr, y_nbr) for core in (c, 1 - c)] + [partner]
 
+    chip = me // 2
+    chips = [base // 2 for base in (diagonal, x_nbr, y_nbr)]
+
     def remote(src, dst, send, recv, dev):
         return pltpu.make_async_remote_copy(
             src_ref=src, dst_ref=dst, send_sem=send, recv_sem=recv,
@@ -94,14 +97,20 @@
         rng = pl.ds(k * CHUNK, CHUNK)
         return pltpu.make_async_copy(w.at[rng], w_out.at[rng], w_in.at[k])
 
+    def swap_copies(g):
+        slot = g % GSLOTS
+        return [remote(swap, stage.at[slot, :, c], swap_s.at[0], swap_r.at[g, 0], partner),
+                remote(nswap, nstage.at[slot, :, c], swap_s.at[1], swap_r.at[g, 1], partner)]
+
     def own_send(g, r):
         slot = g % GSLOTS
-        return remote(stage.at[slot, peers[r]], owned.at[g % OSLOTS, :, pl.ds(me * rows, rows)],
-                      own_s.at[slot, r], own_r.at[g, r], peers[r])
+        return remote(stage.at[slot, chips[r]], owned.at[g % OSLOTS, pl.ds(chip * 2, 2)],
+                      own_s.at[slot, r], own_r.at[g, r], chips[r] * 2 + c)
 
     def nrm_send(g, r):
         slot = g % GSLOTS
-        return remote(nstage.at[slot, peers[r]], owned_n.at[g, me], nrm_s.at[slot, r], nrm_r.at[g, r], peers[r])
+        return remote(nstage.at[slot, chips[r]], owned_n.at[g, pl.ds(chip * 2, 2)],
+                      nrm_s.at[slot, r], nrm_r.at[g, r], chips[r] * 2 + c)
 
     def back_send(g, r):
         slot = g % XSLOTS
@@ -161,28 +170,38 @@
         for s in range(2):
             part_copy(k, s).wait_recv()
 
-        @pl.when((i == 0) & (g >= GSLOTS))
-        def _():
-            for r in range(NDEV - 1):
-                own_send(g - GSLOTS, r).wait_send()
-                nrm_send(g - GSLOTS, r).wait_send()
-
-        @pl.loop(0, CHUNK)
-        def _(j):
+        def momentum(j):
             new = MOMENTUM_COEF * momb[slot, j] + (kept[k % 2, j] + mom_out[k * CHUNK + j])
             mom_out[k * CHUNK + j] = new
-            stage[gslot, j, i] = new.astype(jnp.bfloat16)
             sq = jnp.sum(new * new, axis=0, keepdims=True)
-            nstage[gslot, j, i] = (sq[:, :128] + sq[:, 128:256]) + (sq[:, 256:384] + sq[:, 384:])
+            return new.astype(jnp.bfloat16), (sq[:, :128] + sq[:, 128:256]) + (sq[:, 256:384] + sq[:, 384:])
+
+        @pl.loop(0, NDEV // 2)
+        def _(q):
+            stage[gslot, q, c, i], nstage[gslot, q, c, i] = momentum(2 * q + c)
+            swap[q, i], nswap[q, i] = momentum(2 * q + 1 - c)
 
         @pl.when(i == GROUP - 1)
         def _():
-            for r in range(NDEV - 1):
+            @pl.when(g >= 1)
+            def _():
+                for r in range(3):
+                    own_send(g - 1, r).wait_send()
+                    nrm_send(g - 1, r).wait_send()
+
+            for copy in swap_copies(g):
+                copy.start()
+            for copy in swap_copies(g):
+                copy.wait()
+            for r in range(3):
                 own_send(g, r).start()
                 nrm_send(g, r).start()
 
-        owned[g % OSLOTS, i, pl.ds(pl.multiple_of(me * rows, rows), rows)] = stage[gslot, me, i]
-        owned_n[g, me, i] = nstage[gslot, me, i]
+            @pl.loop(0, GROUP)
+            def _(n):
+                for core in range(2):
+                    owned[g % OSLOTS, chip * 2 + core, n] = stage[gslot, chip, core, n]
+                    owned_n[g, chip * 2 + core, n] = nstage[gslot, chip, core, n]
 
         @pl.when(k + 1 < steps)
         def _():
@@ -194,7 +213,7 @@
             for r in range(NDEV - 1):
                 back_send(g - XSLOTS, r).wait_send()
 
-        for r in range(NDEV - 1):
+        for r in range(3):
             own_send(g, r).wait_recv()
             nrm_send(g, r).wait_recv()
 
@@ -208,7 +227,7 @@
         @pl.loop(0, NDEV)
         def _(j):
             blk = pl.ds(pl.multiple_of(j * rows, rows), rows)
-            xbuf[slot, i, blk] = (owned[g % OSLOTS, i, blk].astype(jnp.float32) / den).astype(jnp.bfloat16)
+            xbuf[slot, i, blk] = (owned[g % OSLOTS, j, i].astype(jnp.float32) / den).astype(jnp.bfloat16)
 
         @pl.loop(0, NS_ITERS)
         def _(_):
@@ -318,11 +337,9 @@
         for s in range(2):
             part_copy(k, s).wait_send()
 
-    @pl.loop(groups - GSLOTS, groups)
-    def _(g):
-        for r in range(NDEV - 1):
-            own_send(g, r).wait_send()
-            nrm_send(g, r).wait_send()
+    for r in range(3):
+        own_send(last, r).wait_send()
+        nrm_send(last, r).wait_send()
 
     @pl.loop((steps - 4 - GROUP) // GROUP, last)
     def _(g):
@@ -378,9 +395,11 @@
                 pltpu.VMEM((2, CHUNK, rows, n_cols), f32),
                 pltpu.VMEM((SLOTS, 2, HALF, rows, n_cols), f32),
                 pltpu.VMEM((SLOTS, CHUNK, rows, n_cols), f32),
-                pltpu.VMEM((GSLOTS, NDEV, GROUP, rows, n_cols), bf16),
-                pltpu.VMEM((OSLOTS, GROUP, n_rows, n_cols), bf16),
-                pltpu.VMEM((GSLOTS, NDEV, GROUP, 1, 128), f32),
+                pltpu.VMEM((GSLOTS, NDEV // 2, 2, GROUP, rows, n_cols), bf16),
+                pltpu.VMEM((NDEV // 2, GROUP, rows, n_cols), bf16),
+                pltpu.VMEM((OSLOTS, NDEV, GROUP, rows, n_cols), bf16),
+                pltpu.VMEM((GSLOTS, NDEV // 2, 2, GROUP, 1, 128), f32),
+                pltpu.VMEM((NDEV // 2, GROUP, 1, 128), f32),
                 pltpu.VMEM((groups, NDEV, GROUP, 1, 128), f32),
                 pltpu.VMEM((XSLOTS, GROUP, n_rows, n_cols), bf16),
                 pltpu.VMEM((RSLOTS, NDEV, GROUP, rows, n_cols), bf16),
@@ -388,8 +407,9 @@
                 pltpu.VMEM((n_rows, n_rows), bf16),
                 dma((steps // PAIR, 2, 3)), dma((steps // PAIR, 2, 3)),
                 dma((SLOTS, 2)), dma((steps, 2)),
-                dma((GSLOTS, NDEV)), dma((groups, NDEV)),
-                dma((GSLOTS, NDEV)), dma((groups, NDEV)),
+                dma((2,)), dma((groups, 2)),
+                dma((GSLOTS, 3)), dma((groups, 3)),
+                dma((GSLOTS, 3)), dma((groups, 3)),
                 dma((XSLOTS, NDEV)), dma((groups, NDEV)),
                 dma((GROUP, NDEV)), dma((GROUP, NDEV)),
                 dma((2, 4)), dma((SLOTS,)), dma((steps,)),

time: 742 us -> 741 us (level)
  no operation moved by 1% of the time
where the time goes in v6:
time: 741 us; the launch traced here: 740 us
  Pallas kernels  740 us (100%)
    pallas_call x1, Pallas kernels, local_step(): pl.pallas_call(muon_kernel, name='muon_step', out_shape=(pltpu.VMEM((2, n...  729 us

profile of v6, /device:TPU:0, one launch (start us, length us, event | category | flops | bytes accessed | tf_op | source)
XLA Modules:
  0.0 740.4 jit_solution(5999635084669712639)
XLA Ops:
  0.6 728.7 %muon_step.1 = (f32[2,128,64,512]{3,2,1,0:T(8,128)S(1)}, bf16[8,2,3,2,4,2,64,512]{7,6,5,4,3,2,1,0:T(8,128)(2,1)}) custom-call(bf16[16,2,4,2,2,2,64,512]{7,6,5,4,3,2,1,0:T(8,128)(2,1)} %bitcast.grad, f32[128,64,512]{2,1,0:T(8,128)} %mom.1, f32[128,64,512]{2,1,0:T(8,128)} %w.1), custom_call_target="tpu_custom_call" | custom-call | tf_op jit(solution)/shard_map/muon_step/pallas_call | solution.py:384
  729.3 11.0 %write_results.1 = (f32[128,64,512]{2,1,0:T(8,128)}, f32[128,64,512]{2,1,0:T(8,128)}) custom-call(f32[2,128,64,512]{3,2,1,0:T(8,128)S(1)} %get-tuple-element.3.results), custom_call_target="tpu_custom_call" | custom-call | tf_op jit(solution)/shard_map/write_results/pallas_call | solution.py:420

commit v7 on v6

--- a/solution.py
+++ b/solution.py
@@ -34,8 +34,8 @@
 
 def muon_kernel(
     grad, mom, w, results, raw,
-    inbuf, kept, part, momb, stage, swap, owned, nstage, nswap, owned_n, xbuf, xin, gram, poly,
-    raw_s, raw_r, part_s, part_r, swap_s, swap_r, own_s, own_r, nrm_s, nrm_r, back_s, back_r, tail_s, tail_r,
+    inbuf, kept, part, momb, stage, swap, owned, nstage, nswap, owned_n, xbuf, xswap, xstage, xin, gram, poly,
+    raw_s, raw_r, part_s, part_r, swap_s, swap_r, own_s, own_r, nrm_s, nrm_r, xswap_s, xswap_r, back_s, back_r, tswap_s, tswap_r, tail_s, tail_r,
     in_sem, mom_in, w_in,
 ):
     n_mats, rows, cols = mom.shape
@@ -112,15 +112,24 @@
         return remote(nstage.at[slot, chips[r]], owned_n.at[g, pl.ds(chip * 2, 2)],
                       nrm_s.at[slot, r], nrm_r.at[g, r], chips[r] * 2 + c)
 
+    def xswap_copy(g):
+        return remote(xswap, xstage.at[g % XSLOTS, :, c], xswap_s.at[0], xswap_r.at[g], partner)
+
     def back_send(g, r):
         slot = g % XSLOTS
-        return remote(xbuf.at[slot, :, pl.ds(peers[r] * rows, rows)], xin.at[g % RSLOTS, me],
-                      back_s.at[slot, r], back_r.at[g, r], peers[r])
+        return remote(xstage.at[slot, chips[r]], xin.at[g % RSLOTS, pl.ds(chip * 2, 2)],
+                      back_s.at[slot, r], back_r.at[g, r], chips[r] * 2 + c)
+
+    def tail_swap(g, i):
+        return remote(xswap.at[:, i], xstage.at[g % XSLOTS, :, c, i], tswap_s.at[i], tswap_r.at[i], partner)
 
     def tail_send(g, i, r):
-        slot = g % XSLOTS
-        return remote(xbuf.at[slot, i, pl.ds(peers[r] * rows, rows)], xin.at[g % RSLOTS, me, i],
-                      tail_s.at[i, r], tail_r.at[i, r], peers[r])
+        return remote(xstage.at[g % XSLOTS, chips[r], :, i], xin.at[g % RSLOTS, pl.ds(chip * 2, 2), i],
+                      tail_s.at[i, r], tail_r.at[i, r], chips[r] * 2 + c)
+
+    def keep_rows(g, i):
+        for core in range(2):
+            xin[g % RSLOTS, chip * 2 + core, i] = xstage[g % XSLOTS, chip, core, i]
 
     def sum_chunk(k):
         slot = k % SLOTS
@@ -189,6 +198,11 @@
                     own_send(g - 1, r).wait_send()
                     nrm_send(g - 1, r).wait_send()
 
+            @pl.when(g >= XSLOTS)
+            def _():
+                for r in range(3):
+                    back_send(g - XSLOTS, r).wait_send()
+
             for copy in swap_copies(g):
                 copy.start()
             for copy in swap_copies(g):
@@ -208,17 +222,11 @@
             mom_load(k + 1).start()
 
     def owned_arrival(g):
-        @pl.when(g >= XSLOTS)
-        def _():
-            for r in range(NDEV - 1):
-                back_send(g - XSLOTS, r).wait_send()
-
         for r in range(3):
             own_send(g, r).wait_recv()
             nrm_send(g, r).wait_recv()
 
     def orthogonalize(g, i):
-        slot = g % XSLOTS
         sq = owned_n[g, 0, i]
         for j in range(1, NDEV):
             sq = sq + owned_n[g, j, i]
@@ -227,24 +235,32 @@
         @pl.loop(0, NDEV)
         def _(j):
             blk = pl.ds(pl.multiple_of(j * rows, rows), rows)
-            xbuf[slot, i, blk] = (owned[g % OSLOTS, j, i].astype(jnp.float32) / den).astype(jnp.bfloat16)
+            xbuf[blk] = (owned[g % OSLOTS, j, i].astype(jnp.float32) / den).astype(jnp.bfloat16)
 
         @pl.loop(0, NS_ITERS)
         def _(_):
-            cur = xbuf[slot, i]
+            cur = xbuf[...]
             gram[...] = lax.dot_general(cur, cur, (((1,), (1,)), ((), ())),
                                         preferred_element_type=jnp.float32).astype(jnp.bfloat16)
             gm = gram[...]
             sqr = jnp.dot(gm, gm, preferred_element_type=jnp.float32)
             poly[...] = (COEF_B * gm.astype(jnp.float32) + COEF_C * sqr).astype(jnp.bfloat16)
             px = jnp.dot(poly[...], cur, preferred_element_type=jnp.float32)
-            xbuf[slot, i] = (COEF_A * cur.astype(jnp.float32) + px).astype(jnp.bfloat16)
-
-        xin[g % RSLOTS, me, i] = xbuf[slot, i, pl.ds(pl.multiple_of(me * rows, rows), rows)]
+            xbuf[...] = (COEF_A * cur.astype(jnp.float32) + px).astype(jnp.bfloat16)
+
+        @pl.loop(0, NDEV // 2)
+        def _(q):
+            xstage[g % XSLOTS, q, c, i] = xbuf[pl.ds(pl.multiple_of((2 * q + c) * rows, rows), rows)]
+            xswap[q, i] = xbuf[pl.ds(pl.multiple_of((2 * q + 1 - c) * rows, rows), rows)]
 
     def send_back(g):
-        for r in range(NDEV - 1):
+        xswap_copy(g).wait()
+        for r in range(3):
             back_send(g, r).start()
+
+        @pl.loop(0, GROUP)
+        def _(i):
+            keep_rows(g, i)
 
     def update_rows(g, i, j):
         m = (g * GROUP + i) * CHUNK + j
@@ -255,24 +271,24 @@
     def update_weights(g):
         for i in range(GROUP):
             w_load(g * GROUP + i).wait()
-        for r in range(NDEV):
-            j = peers[r] if r < NDEV - 1 else me
-            if r < NDEV - 1:
-                pltpu.make_async_copy(xin.at[g % RSLOTS, j], xin.at[g % RSLOTS, j], back_r.at[g, r]).wait()
+        for r in range(4):
+            if r < 3:
+                back_send(g, r).wait_recv()
 
             @pl.loop(0, GROUP)
             def _(i):
-                update_rows(g, i, j)
+                for core in range(2):
+                    update_rows(g, i, (chips + [chip])[r] * 2 + core)
 
     def update_last(g):
         @pl.loop(0, GROUP)
         def _(i):
             w_load(g * GROUP + i).wait()
-            update_rows(g, i, me)
-            for r in range(NDEV - 1):
-                pltpu.make_async_copy(xin.at[g % RSLOTS, peers[r], i], xin.at[g % RSLOTS, peers[r], i],
-                                      tail_r.at[i, r]).wait()
-                update_rows(g, i, peers[r])
+            for r in range(-1, 3):
+                if r >= 0:
+                    tail_send(g, i, r).wait_recv()
+                for core in range(2):
+                    update_rows(g, i, (chips[r] if r >= 0 else chip) * 2 + core)
 
     for q in range(AHEAD // PAIR):
         for copy in raw_copies(q):
@@ -305,7 +321,12 @@
 
         @pl.when(t >= 1 + GROUP)
         def _():
-            orthogonalize((t - 1) // GROUP - 1, (t - 1) % GROUP)
+            g, i = (t - 1) // GROUP - 1, (t - 1) % GROUP
+            orthogonalize(g, i)
+
+            @pl.when(i == GROUP - 1)
+            def _():
+                xswap_copy(g).start()
 
         at(3 + GROUP, update_weights)
 
@@ -322,10 +343,18 @@
 
         orthogonalize(last - 1 + n // GROUP, n % GROUP)
 
+        @pl.when(n == GROUP - 1)
+        def _():
+            xswap_copy(last - 1).start()
+
         @pl.when(n >= GROUP)
         def _():
-            for r in range(NDEV - 1):
-                tail_send(last, n - GROUP, r).start()
+            i = n - GROUP
+            tail_swap(last, i).start()
+            tail_swap(last, i).wait()
+            for r in range(3):
+                tail_send(last, i, r).start()
+            keep_rows(last, i)
 
     @pl.loop(0, steps // PAIR)
     def _(q):
@@ -347,7 +376,7 @@
 
     update_last(last)
 
-    for r in range(NDEV - 1):
+    for r in range(3):
         for g in range(groups - XSLOTS, last):
             back_send(g, r).wait_send()
         for i in range(GROUP):
@@ -401,7 +430,9 @@
                 pltpu.VMEM((GSLOTS, NDEV // 2, 2, GROUP, 1, 128), f32),
                 pltpu.VMEM((NDEV // 2, GROUP, 1, 128), f32),
                 pltpu.VMEM((groups, NDEV, GROUP, 1, 128), f32),
-                pltpu.VMEM((XSLOTS, GROUP, n_rows, n_cols), bf16),
+                pltpu.VMEM((n_rows, n_cols), bf16),
+                pltpu.VMEM((NDEV // 2, GROUP, rows, n_cols), bf16),
+                pltpu.VMEM((XSLOTS, NDEV // 2, 2, GROUP, rows, n_cols), bf16),
                 pltpu.VMEM((RSLOTS, NDEV, GROUP, rows, n_cols), bf16),
                 pltpu.VMEM((n_rows, n_rows), bf16),
                 pltpu.VMEM((n_rows, n_rows), bf16),
@@ -410,8 +441,10 @@
                 dma((2,)), dma((groups, 2)),
                 dma((GSLOTS, 3)), dma((groups, 3)),
                 dma((GSLOTS, 3)), dma((groups, 3)),
-                dma((XSLOTS, NDEV)), dma((groups, NDEV)),
-                dma((GROUP, NDEV)), dma((GROUP, NDEV)),
+                dma((1,)), dma((groups,)),
+                dma((XSLOTS, 3)), dma((groups, 3)),
+                dma((GROUP,)), dma((GROUP,)),
+                dma((GROUP, 3)), dma((GROUP, 3)),
                 dma((2, 4)), dma((SLOTS,)), dma((steps,)),
             ],
             compiler_params=pltpu.CompilerParams(

time: 741 us -> 744 us (level)
  no operation moved by 1% of the time
where the time goes in v7:
time: 744 us
  Pallas kernels  743 us (100%)
    pallas_call x1, Pallas kernels, local_step(): pl.pallas_call(muon_kernel, name='muon_step', out_shape=(pltpu.VMEM((2, n...  732 us

profile of v7, /device:TPU:0, one launch (start us, length us, event | category | flops | bytes accessed | tf_op | source)
XLA Modules:
  0.0 743.8 jit_solution(16673172402681396788)
XLA Ops:
  0.6 732.1 %muon_step.1 = (f32[2,128,64,512]{3,2,1,0:T(8,128)S(1)}, bf16[8,2,3,2,4,2,64,512]{7,6,5,4,3,2,1,0:T(8,128)(2,1)}) custom-call(bf16[16,2,4,2,2,2,64,512]{7,6,5,4,3,2,1,0:T(8,128)(2,1)} %bitcast.grad, f32[128,64,512]{2,1,0:T(8,128)} %mom.1, f32[128,64,512]{2,1,0:T(8,128)} %w.1), custom_call_target="tpu_custom_call" | custom-call | tf_op jit(solution)/shard_map/muon_step/pallas_call | solution.py:413
  732.8 11.0 %write_results.1 = (f32[128,64,512]{2,1,0:T(8,128)}, f32[128,64,512]{2,1,0:T(8,128)}) custom-call(f32[2,128,64,512]{3,2,1,0:T(8,128)S(1)} %get-tuple-element.3.results), custom_call_target="tpu_custom_call" | custom-call | tf_op jit(solution)/shard_map/write_results/pallas_call | solution.py:453

commit v8 on v7

--- a/solution.py
+++ b/solution.py
@@ -35,7 +35,7 @@
 def muon_kernel(
     grad, mom, w, results, raw,
     inbuf, kept, part, momb, stage, swap, owned, nstage, nswap, owned_n, xbuf, xswap, xstage, xin, gram, poly,
-    raw_s, raw_r, part_s, part_r, swap_s, swap_r, own_s, own_r, nrm_s, nrm_r, xswap_s, xswap_r, back_s, back_r, tswap_s, tswap_r, tail_s, tail_r,
+    raw_s, raw_r, part_s, part_r, swap_s, swap_r, own_s, own_r, nrm_s, nrm_r, xswap_s, xswap_r, back_s, back_r, tail_s, tail_r,
     in_sem, mom_in, w_in,
 ):
     n_mats, rows, cols = mom.shape
@@ -120,16 +120,9 @@
         return remote(xstage.at[slot, chips[r]], xin.at[g % RSLOTS, pl.ds(chip * 2, 2)],
                       back_s.at[slot, r], back_r.at[g, r], chips[r] * 2 + c)
 
-    def tail_swap(g, i):
-        return remote(xswap.at[:, i], xstage.at[g % XSLOTS, :, c, i], tswap_s.at[i], tswap_r.at[i], partner)
-
     def tail_send(g, i, r):
-        return remote(xstage.at[g % XSLOTS, chips[r], :, i], xin.at[g % RSLOTS, pl.ds(chip * 2, 2), i],
-                      tail_s.at[i, r], tail_r.at[i, r], chips[r] * 2 + c)
-
-    def keep_rows(g, i):
-        for core in range(2):
-            xin[g % RSLOTS, chip * 2 + core, i] = xstage[g % XSLOTS, chip, core, i]
+        return remote(xbuf.at[i, pl.ds(peers[r] * rows, rows)], xin.at[g % RSLOTS, me, i],
+                      tail_s.at[i, r], tail_r.at[i, r], peers[r])
 
     def sum_chunk(k):
         slot = k % SLOTS
@@ -235,23 +228,28 @@
         @pl.loop(0, NDEV)
         def _(j):
             blk = pl.ds(pl.multiple_of(j * rows, rows), rows)
-            xbuf[blk] = (owned[g % OSLOTS, j, i].astype(jnp.float32) / den).astype(jnp.bfloat16)
+            xbuf[i, blk] = (owned[g % OSLOTS, j, i].astype(jnp.float32) / den).astype(jnp.bfloat16)
 
         @pl.loop(0, NS_ITERS)
         def _(_):
-            cur = xbuf[...]
+            cur = xbuf[i]
             gram[...] = lax.dot_general(cur, cur, (((1,), (1,)), ((), ())),
                                         preferred_element_type=jnp.float32).astype(jnp.bfloat16)
             gm = gram[...]
             sqr = jnp.dot(gm, gm, preferred_element_type=jnp.float32)
             poly[...] = (COEF_B * gm.astype(jnp.float32) + COEF_C * sqr).astype(jnp.bfloat16)
             px = jnp.dot(poly[...], cur, preferred_element_type=jnp.float32)
-            xbuf[...] = (COEF_A * cur.astype(jnp.float32) + px).astype(jnp.bfloat16)
-
+            xbuf[i] = (COEF_A * cur.astype(jnp.float32) + px).astype(jnp.bfloat16)
+
+    def split_rows(g, i):
         @pl.loop(0, NDEV // 2)
         def _(q):
-            xstage[g % XSLOTS, q, c, i] = xbuf[pl.ds(pl.multiple_of((2 * q + c) * rows, rows), rows)]
-            xswap[q, i] = xbuf[pl.ds(pl.multiple_of((2 * q + 1 - c) * rows, rows), rows)]
+            xstage[g % XSLOTS, q, c, i] = xbuf[i, pl.ds(pl.multiple_of((2 * q + c) * rows, rows), rows)]
+            xswap[q, i] = xbuf[i, pl.ds(pl.multiple_of((2 * q + 1 - c) * rows, rows), rows)]
+
+        @pl.when(i == GROUP - 1)
+        def _():
+            xswap_copy(g).start()
 
     def send_back(g):
         xswap_copy(g).wait()
@@ -260,7 +258,8 @@
 
         @pl.loop(0, GROUP)
         def _(i):
-            keep_rows(g, i)
+            for core in range(2):
+                xin[g % RSLOTS, chip * 2 + core, i] = xstage[g % XSLOTS, chip, core, i]
 
     def update_rows(g, i, j):
         m = (g * GROUP + i) * CHUNK + j
@@ -284,11 +283,11 @@
         @pl.loop(0, GROUP)
         def _(i):
             w_load(g * GROUP + i).wait()
-            for r in range(-1, 3):
-                if r >= 0:
-                    tail_send(g, i, r).wait_recv()
-                for core in range(2):
-                    update_rows(g, i, (chips[r] if r >= 0 else chip) * 2 + core)
+            update_rows(g, i, me)
+            for r in range(NDEV - 1):
+                pltpu.make_async_copy(xin.at[g % RSLOTS, peers[r], i], xin.at[g % RSLOTS, peers[r], i],
+                                      tail_r.at[i, r]).wait()
+                update_rows(g, i, peers[r])
 
     for q in range(AHEAD // PAIR):
         for copy in raw_copies(q):
@@ -323,10 +322,7 @@
         def _():
             g, i = (t - 1) // GROUP - 1, (t - 1) % GROUP
             orthogonalize(g, i)
-
-            @pl.when(i == GROUP - 1)
-            def _():
-                xswap_copy(g).start()
+            split_rows(g, i)
 
         at(3 + GROUP, update_weights)
 
@@ -345,16 +341,14 @@
 
         @pl.when(n == GROUP - 1)
         def _():
-            xswap_copy(last - 1).start()
+            split_rows(last - 1, n)
 
         @pl.when(n >= GROUP)
         def _():
             i = n - GROUP
-            tail_swap(last, i).start()
-            tail_swap(last, i).wait()
-            for r in range(3):
+            for r in range(NDEV - 1):
                 tail_send(last, i, r).start()
-            keep_rows(last, i)
+            xin[last % RSLOTS, me, i] = xbuf[i, pl.ds(pl.multiple_of(me * rows, rows), rows)]
 
     @pl.loop(0, steps // PAIR)
     def _(q):
@@ -376,10 +370,11 @@
 
     update_last(last)
 
-    for r in range(3):
-        for g in range(groups - XSLOTS, last):
+    for g in range(groups - XSLOTS, last):
+        for r in range(3):
             back_send(g, r).wait_send()
-        for i in range(GROUP):
+    for i in range(GROUP):
+        for r in range(NDEV - 1):
             tail_send(last, i, r).wait_send()
 
 
@@ -430,7 +425,7 @@
                 pltpu.VMEM((GSLOTS, NDEV // 2, 2, GROUP, 1, 128), f32),
                 pltpu.VMEM((NDEV // 2, GROUP, 1, 128), f32),
                 pltpu.VMEM((groups, NDEV, GROUP, 1, 128), f32),
-                pltpu.VMEM((n_rows, n_cols), bf16),
+                pltpu.VMEM((GROUP, n_rows, n_cols), bf16),
                 pltpu.VMEM((NDEV // 2, GROUP, rows, n_cols), bf16),
                 pltpu.VMEM((XSLOTS, NDEV // 2, 2, GROUP, rows, n_cols), bf16),
                 pltpu.VMEM((RSLOTS, NDEV, GROUP, rows, n_cols), bf16),
@@ -443,8 +438,7 @@
                 dma((GSLOTS, 3)), dma((groups, 3)),
                 dma((1,)), dma((groups,)),
                 dma((XSLOTS, 3)), dma((groups, 3)),
-                dma((GROUP,)), dma((GROUP,)),
-                dma((GROUP, 3)), dma((GROUP, 3)),
+                dma((GROUP, NDEV)), dma((GROUP, NDEV)),
                 dma((2, 4)), dma((SLOTS,)), dma((steps,)),
             ],
             compiler_params=pltpu.CompilerParams(

time: 744 us -> 740 us (level)
  no operation moved by 1% of the time
where the time goes in v8:
time: 740 us
  Pallas kernels  739 us (100%)
    pallas_call x1, Pallas kernels, local_step(): pl.pallas_call(muon_kernel, name='muon_step', out_shape=(pltpu.VMEM((2, n...  728 us

profile of v8, /device:TPU:0, one launch (start us, length us, event | category | flops | bytes accessed | tf_op | source)
XLA Modules:
  0.0 739.9 jit_solution(10829031469402570300)
XLA Ops:
  0.6 728.3 %muon_step.1 = (f32[2,128,64,512]{3,2,1,0:T(8,128)S(1)}, bf16[8,2,3,2,4,2,64,512]{7,6,5,4,3,2,1,0:T(8,128)(2,1)}) custom-call(bf16[16,2,4,2,2,2,64,512]{7,6,5,4,3,2,1,0:T(8,128)(2,1)} %bitcast.grad, f32[128,64,512]{2,1,0:T(8,128)} %mom.1, f32[128,64,512]{2,1,0:T(8,128)} %w.1), custom_call_target="tpu_custom_call" | custom-call | tf_op jit(solution)/shard_map/muon_step/pallas_call | solution.py:408
  728.9 11.0 %write_results.1 = (f32[128,64,512]{2,1,0:T(8,128)}, f32[128,64,512]{2,1,0:T(8,128)}) custom-call(f32[2,128,64,512]{3,2,1,0:T(8,128)S(1)} %get-tuple-element.3.results), custom_call_target="tpu_custom_call" | custom-call | tf_op jit(solution)/shard_map/write_results/pallas_call | solution.py:447

commit v9 on v8

--- a/solution.py
+++ b/solution.py
@@ -20,8 +20,8 @@
 NDEV = 8
 CHUNK = 8
 HALF = 4
-PAIR = 2
-AHEAD = 2
+PAIR = 4
+AHEAD = 4
 SLOTS = 3
 GROUP = 2
 GSLOTS = 2

time: 740 us -> 740 us (level)
  no operation moved by 1% of the time
where the time goes in v9:
time: 740 us
  Pallas kernels  739 us (100%)
    pallas_call x1, Pallas kernels, local_step(): pl.pallas_call(muon_kernel, name='muon_step', out_shape=(pltpu.VMEM((2, n...  728 us

profile of v9, /device:TPU:0, one launch (start us, length us, event | category | flops | bytes accessed | tf_op | source)
XLA Modules:
  0.0 739.5 jit_solution(7168981963372891843)
XLA Ops:
  0.6 727.8 %muon_step.1 = (f32[2,128,64,512]{3,2,1,0:T(8,128)S(1)}, bf16[4,2,3,4,4,2,64,512]{7,6,5,4,3,2,1,0:T(8,128)(2,1)}) custom-call(bf16[16,2,4,2,2,2,64,512]{7,6,5,4,3,2,1,0:T(8,128)(2,1)} %bitcast.grad, f32[128,64,512]{2,1,0:T(8,128)} %mom.1, f32[128,64,512]{2,1,0:T(8,128)} %w.1), custom_call_target="tpu_custom_call" | custom-call | tf_op jit(solution)/shard_map/muon_step/pallas_call | solution.py:408
  728.5 11.0 %write_results.1 = (f32[128,64,512]{2,1,0:T(8,128)}, f32[128,64,512]{2,1,0:T(8,128)}) custom-call(f32[2,128,64,512]{3,2,1,0:T(8,128)S(1)} %get-tuple-element.3.results), custom_call_target="tpu_custom_call" | custom-call | tf_op jit(solution)/shard_map/write_results/pallas_call | solution.py:447

commit v10 on v9

--- a/solution.py
+++ b/solution.py
@@ -25,9 +25,9 @@
 SLOTS = 3
 GROUP = 2
 GSLOTS = 2
-OSLOTS = 3
+OSLOTS = 4
 XSLOTS = 3
-RSLOTS = 3
+RSLOTS = 4
 PIECES = 4
 MESH = pl.DeviceIdType.MESH
 
@@ -35,7 +35,7 @@
 def muon_kernel(
     grad, mom, w, results, raw,
     inbuf, kept, part, momb, stage, swap, owned, nstage, nswap, owned_n, xbuf, xswap, xstage, xin, gram, poly,
-    raw_s, raw_r, part_s, part_r, swap_s, swap_r, own_s, own_r, nrm_s, nrm_r, xswap_s, xswap_r, back_s, back_r, tail_s, tail_r,
+    raw_s, raw_r, part_s, part_r, swap_s, swap_r, own_s, own_r, nrm_s, nrm_r, xswap_s, xswap_r, back_s, back_r, tail_s, tail_r, lswap_s, lswap_r, lown_s, lown_r, lnrm_s, lnrm_r,
     in_sem, mom_in, w_in,
 ):
     n_mats, rows, cols = mom.shape
@@ -112,6 +112,20 @@
         return remote(nstage.at[slot, chips[r]], owned_n.at[g, pl.ds(chip * 2, 2)],
                       nrm_s.at[slot, r], nrm_r.at[g, r], chips[r] * 2 + c)
 
+    final = steps // GROUP - 1
+    fslot = final % GSLOTS
+
+    def last_swap(i):
+        return [remote(swap.at[:, i], stage.at[fslot, :, c, i], lswap_s.at[i, 0], lswap_r.at[i, 0], partner),
+                remote(nswap.at[:, i], nstage.at[fslot, :, c, i], lswap_s.at[i, 1], lswap_r.at[i, 1], partner)]
+
+    def last_send(i, r):
+        dev = chips[r] * 2 + c
+        return [remote(stage.at[fslot, chips[r], :, i], owned.at[final % OSLOTS, pl.ds(chip * 2, 2), i],
+                       lown_s.at[i, r], lown_r.at[i, r], dev),
+                remote(nstage.at[fslot, chips[r], :, i], owned_n.at[final, pl.ds(chip * 2, 2), i],
+                       lnrm_s.at[i, r], lnrm_r.at[i, r], dev)]
+
     def xswap_copy(g):
         return remote(xswap, xstage.at[g % XSLOTS, :, c], xswap_s.at[0], xswap_r.at[g], partner)
 
@@ -183,7 +197,23 @@
             stage[gslot, q, c, i], nstage[gslot, q, c, i] = momentum(2 * q + c)
             swap[q, i], nswap[q, i] = momentum(2 * q + 1 - c)
 
-        @pl.when(i == GROUP - 1)
+        def keep_rows(n):
+            for core in range(2):
+                owned[g % OSLOTS, chip * 2 + core, n] = stage[gslot, chip, core, n]
+                owned_n[g, chip * 2 + core, n] = nstage[gslot, chip, core, n]
+
+        @pl.when(g == final)
+        def _():
+            for copy in last_swap(i):
+                copy.start()
+            for copy in last_swap(i):
+                copy.wait()
+            for r in range(3):
+                for copy in last_send(i, r):
+                    copy.start()
+            keep_rows(i)
+
+        @pl.when((i == GROUP - 1) & (g < final))
         def _():
             @pl.when(g >= 1)
             def _():
@@ -206,9 +236,7 @@
 
             @pl.loop(0, GROUP)
             def _(n):
-                for core in range(2):
-                    owned[g % OSLOTS, chip * 2 + core, n] = stage[gslot, chip, core, n]
-                    owned_n[g, chip * 2 + core, n] = nstage[gslot, chip, core, n]
+                keep_rows(n)
 
         @pl.when(k + 1 < steps)
         def _():
@@ -335,7 +363,12 @@
         @pl.when(n == GROUP)
         def _():
             send_back(last - 1)
-            owned_arrival(last)
+
+        @pl.when(n >= GROUP)
+        def _():
+            for r in range(3):
+                for copy in last_send(n - GROUP, r):
+                    copy.wait_recv()
 
         orthogonalize(last - 1 + n // GROUP, n % GROUP)
 
@@ -361,8 +394,11 @@
             part_copy(k, s).wait_send()
 
     for r in range(3):
-        own_send(last, r).wait_send()
-        nrm_send(last, r).wait_send()
+        own_send(last - 1, r).wait_send()
+        nrm_send(last - 1, r).wait_send()
+        for i in range(GROUP):
+            for copy in last_send(i, r):
+                copy.wait_send()
 
     @pl.loop((steps - 4 - GROUP) // GROUP, last)
     def _(g):
@@ -370,7 +406,7 @@
 
     update_last(last)
 
-    for g in range(groups - XSLOTS, last):
+    for g in range(last - XSLOTS, last):
         for r in range(3):
             back_send(g, r).wait_send()
     for i in range(GROUP):
@@ -439,6 +475,7 @@
                 dma((1,)), dma((groups,)),
                 dma((XSLOTS, 3)), dma((groups, 3)),
                 dma((GROUP, NDEV)), dma((GROUP, NDEV)),
+                *[dma((GROUP, 3))] * 6,
                 dma((2, 4)), dma((SLOTS,)), dma((steps,)),
             ],
             compiler_params=pltpu.CompilerParams(

time: 740 us -> 740 us (level)
  no operation moved by 1% of the time
where the time goes in v10:
time: 740 us
  Pallas kernels  739 us (100%)
    pallas_call x1, Pallas kernels, local_step(): pl.pallas_call(muon_kernel, name='muon_step', out_shape=(pltpu.VMEM((2, n...  728 us

profile of v10, /device:TPU:0, one launch (start us, length us, event | category | flops | bytes accessed | tf_op | source)
XLA Modules:
  0.0 739.9 jit_solution(8288368008163513230)
XLA Ops:
  0.6 728.2 %muon_step.1 = (f32[2,128,64,512]{3,2,1,0:T(8,128)S(1)}, bf16[4,2,3,4,4,2,64,512]{7,6,5,4,3,2,1,0:T(8,128)(2,1)}) custom-call(bf16[16,2,4,2,2,2,64,512]{7,6,5,4,3,2,1,0:T(8,128)(2,1)} %bitcast.grad, f32[128,64,512]{2,1,0:T(8,128)} %mom.1, f32[128,64,512]{2,1,0:T(8,128)} %w.1), custom_call_target="tpu_custom_call" | custom-call | tf_op jit(solution)/shard_map/muon_step/pallas_call | solution.py:444
  728.8 11.0 %write_results.1 = (f32[128,64,512]{2,1,0:T(8,128)}, f32[128,64,512]{2,1,0:T(8,128)}) custom-call(f32[2,128,64,512]{3,2,1,0:T(8,128)S(1)} %get-tuple-element.3.results), custom_call_target="tpu_custom_call" | custom-call | tf_op jit(solution)/shard_map/write_results/pallas_call | solution.py:484

commit v11 on v9

--- a/solution.py
+++ b/solution.py
@@ -298,12 +298,15 @@
 
     @pl.loop(0, steps)
     def _(t):
-        @pl.when((t % PAIR == 0) & (t + AHEAD < steps))
-        def _():
-            for copy in raw_copies((t + AHEAD) // PAIR):
-                copy.start()
-
+        def next_raw(core):
+            @pl.when((t % PAIR == 0) & (t + AHEAD < steps) & (c == core))
+            def _():
+                for copy in raw_copies((t + AHEAD) // PAIR):
+                    copy.start()
+
+        next_raw(0)
         sum_chunk(t)
+        next_raw(1)
 
         def at(lag, work):
             @pl.when(((t - lag) % GROUP == 0) & (t >= lag + GROUP))

time: 740 us -> 740 us (level)
  no operation moved by 1% of the time
where the time goes in v11:
time: 740 us
  Pallas kernels  739 us (100%)
    pallas_call x1, Pallas kernels, local_step(): pl.pallas_call(muon_kernel, name='muon_step', out_shape=(pltpu.VMEM((2, n...  728 us

profile of v11, /device:TPU:0, one launch (start us, length us, event | category | flops | bytes accessed | tf_op | source)
XLA Modules:
  0.0 740.1 jit_solution(1230784820895454535)
XLA Ops:
  0.6 728.4 %muon_step.1 = (f32[2,128,64,512]{3,2,1,0:T(8,128)S(1)}, bf16[4,2,3,4,4,2,64,512]{7,6,5,4,3,2,1,0:T(8,128)(2,1)}) custom-call(bf16[16,2,4,2,2,2,64,512]{7,6,5,4,3,2,1,0:T(8,128)(2,1)} %bitcast.grad, f32[128,64,512]{2,1,0:T(8,128)} %mom.1, f32[128,64,512]{2,1,0:T(8,128)} %w.1), custom_call_target="tpu_custom_call" | custom-call | tf_op jit(solution)/shard_map/muon_step/pallas_call | solution.py:411
  729.0 11.0 %write_results.1 = (f32[128,64,512]{2,1,0:T(8,128)}, f32[128,64,512]{2,1,0:T(8,128)}) custom-call(f32[2,128,64,512]{3,2,1,0:T(8,128)S(1)} %get-tuple-element.3.results), custom_call_target="tpu_custom_call" | custom-call | tf_op jit(solution)/shard_map/write_results/pallas_call | solution.py:450

commit v12 on v9

--- a/solution.py
+++ b/solution.py
@@ -28,7 +28,7 @@
 OSLOTS = 3
 XSLOTS = 3
 RSLOTS = 3
-PIECES = 4
+PIECES = 2
 MESH = pl.DeviceIdType.MESH
 
 

time: 740 us -> 740 us (level)
  no operation moved by 1% of the time
where the time goes in v12:
time: 740 us
  Pallas kernels  739 us (100%)
    pallas_call x1, Pallas kernels, local_step(): pl.pallas_call(muon_kernel, name='muon_step', out_shape=(pltpu.VMEM((2, n...  728 us

profile of v12, /device:TPU:0, one launch (start us, length us, event | category | flops | bytes accessed | tf_op | source)
XLA Modules:
  0.0 739.7 jit_solution(14835070325889953750)
XLA Ops:
  0.6 727.8 %muon_step.1 = (f32[2,128,64,512]{3,2,1,0:T(8,128)S(1)}, bf16[4,2,3,4,4,2,64,512]{7,6,5,4,3,2,1,0:T(8,128)(2,1)}) custom-call(bf16[16,2,4,2,2,2,64,512]{7,6,5,4,3,2,1,0:T(8,128)(2,1)} %bitcast.grad, f32[128,64,512]{2,1,0:T(8,128)} %mom.1, f32[128,64,512]{2,1,0:T(8,128)} %w.1), custom_call_target="tpu_custom_call" | custom-call | tf_op jit(solution)/shard_map/muon_step/pallas_call | solution.py:408
  728.5 11.2 %write_results.1 = (f32[128,64,512]{2,1,0:T(8,128)}, f32[128,64,512]{2,1,0:T(8,128)}) custom-call(f32[2,128,64,512]{3,2,1,0:T(8,128)S(1)} %get-tuple-element.3.results), custom_call_target="tpu_custom_call" | custom-call | tf_op jit(solution)/shard_map/write_results/pallas_call | solution.py:447
